TPU v7x, 32 devices: a whole 2x2x4 slice. The times are simulated.
32 devices in a mesh: wide: 8 (over z, x), narrow: 4 (over y, core).
Axes of the slice: x: 2, y: 2, z: 4, core: 2. Of those that a mesh axis runs over, the one named last changes fastest.
Arguments:
- tokens: bfloat16 [24, 4, 256, 768], P('wide', 'narrow'), may hold values from -6 to 6
- condition: bfloat16 [24, 768], P('wide'), may hold values from -6 to 6
- counts: int32 [8], P('wide'), may hold values from 1 to 3, as said below
- w_mod: bfloat16 [768, 4608], replicated, may hold values from -0.21875 to 0.21875
- w_qkv: bfloat16 [768, 2304], replicated, may hold values from -0.21875 to 0.21875
- w_out: bfloat16 [768, 768], replicated, may hold values from -1.75 to 1.75
- w_up: bfloat16 [768, 3072], replicated, may hold values from -0.21875 to 0.21875
- w_down: bfloat16 [3072, 768], replicated, may hold values from -0.109375 to 0.109375
- conv_attn: bfloat16 [768, 9], replicated, may hold values from -2 to 2
- conv_ffn: bfloat16 [3072, 9], replicated, may hold values from -2 to 2
- cotangent: bfloat16 [24, 4, 256, 768], P('wide', 'narrow'), may hold values from -6 to 6
Outputs:
- output: bfloat16 [24, 4, 256, 768], P('wide', 'narrow')
- token_grad: bfloat16 [24, 4, 256, 768], P('wide', 'narrow')
- cond_grad: float32 [24, 768], P('wide')
- mod_grad: float32 [768, 4608], P(('wide', 'narrow'))
- qkv_grad: float32 [768, 2304], P(('wide', 'narrow'))
- proj_grad: float32 [768, 768], P(('wide', 'narrow'))
- up_grad: float32 [768, 3072], P(('wide', 'narrow'))
- down_grad: float32 [3072, 768], P(('wide', 'narrow'))
- conv_attn_grad: float32 [768, 9], P(('wide', 'narrow'))
- conv_ffn_grad: float32 [3072, 9], P(('wide', 'narrow'))
Inputs may be any that keep to these rules, and one draw needn't show every extreme that they name: `counts`: items with index b mod 3 at or above the count of their index of wide are padding; some index of wide holds 3 live items.
All inputs are finite; a program needn't handle non-finite values.
Results may differ from a plain program's by a relative error of at most 0.017.
The roundings to bfloat16 on the way count: a program that leaves them out, or rounds other values in their place, can miss the bound.
Values may be sent and summed in bfloat16 or wider, within the bound.
A program may use at most 192 MiB of HBM per device.

v0:
```python
import math

import jax
import jax.numpy as jnp
from jax import lax
from jax.sharding import PartitionSpec as P

HEADS = 12
HEAD_DIM = 64


epsilon = 1e-06


def from_partner(shard, axis, bit):
    return lax.ppermute(shard, axis, [(i, i ^ 1 << bit) for i in range(lax.axis_size(axis))])


def normed(field_map):
    average = jnp.mean(field_map, -1, keepdims=True)
    centred = field_map - average
    variance = jnp.mean(centred * centred, -1, keepdims=True)
    return centred * lax.rsqrt(variance + epsilon)


def modulate(field_map, shift, scale):
    return normed(field_map) * (1.0 + scale) + shift


def gelu_tanh(field_map):
    return jax.nn.gelu(field_map, approximate=True)


def attn_across(outgoing):
    return from_partner(outgoing, "narrow", 0)


def attn_down(outgoing):
    return from_partner(outgoing, "narrow", 1)


def ffn_across(outgoing):
    return from_partner(outgoing, "narrow", 0)


def ffn_down(outgoing):
    return from_partner(outgoing, "narrow", 1)


def extend(field_map, row_half, col_half, across, down):
    outgoing = jnp.where(col_half == 0, field_map[:, :, -1:], field_map[:, :, :1])
    incoming = across(outgoing)
    zeros_rim = jnp.zeros_like(incoming)
    left_rim = jnp.where(col_half == 1, incoming, zeros_rim)
    right_rim = jnp.where(col_half == 0, incoming, zeros_rim)
    widened = jnp.concatenate([left_rim, field_map, right_rim], 2)
    outgoing = jnp.where(row_half == 0, widened[:, -1:], widened[:, :1])
    incoming = down(outgoing)
    zeros_rim = jnp.zeros_like(incoming)
    top_rim = jnp.where(row_half == 1, incoming, zeros_rim)
    bottom_rim = jnp.where(row_half == 0, incoming, zeros_rim)
    return jnp.concatenate([top_rim, widened, bottom_rim], 1)


def apply_taps(padded, kernel, side_len, flipped):
    summed = jnp.zeros((padded.shape[0], side_len, side_len, padded.shape[3]), jnp.float32)
    weights_f = kernel.astype(jnp.float32)
    for stencil in range(9):
        row_off = stencil // 3
        col_off = stencil % 3
        if flipped:
            row_off = 2 - row_off
            col_off = 2 - col_off
        window = padded[:, row_off : row_off + side_len, col_off : col_off + side_len].astype(
            jnp.float32
        )
        summed = summed + window * weights_f[:, stencil]
    return summed


def tap_grads(padded, grad_map, side_len):
    grad_f = grad_map.astype(jnp.float32)
    columns = []
    for stencil in range(9):
        row_off = stencil // 3
        col_off = stencil % 3
        window = padded[:, row_off : row_off + side_len, col_off : col_off + side_len].astype(
            jnp.float32
        )
        columns.append(jnp.sum(window * grad_f, axis=(0, 1, 2)))
    return jnp.stack(columns, 1)


def to_groups(field_map):
    count, side_len, _, channels = field_map.shape
    quarter = side_len // 2
    pieces = field_map.reshape(count, quarter, 2, quarter, 2, channels).transpose(0, 2, 4, 1, 3, 5)
    pieces = pieces.reshape(count, 4, quarter * quarter, channels)
    incoming = lax.all_to_all(pieces, "narrow", split_axis=1, concat_axis=1, tiled=True)
    return incoming.reshape(count, 4 * quarter * quarter, channels)


def to_quads(group_rows):
    count, rows_all, channels = group_rows.shape
    pieces = group_rows.reshape(count, 4, rows_all // 4, channels)
    incoming = lax.all_to_all(pieces, "narrow", split_axis=1, concat_axis=1, tiled=True)
    quarter = math.isqrt(rows_all // 4)
    incoming = incoming.reshape(count, 2, 2, quarter, quarter, channels).transpose(0, 3, 1, 4, 2, 5)
    return incoming.reshape(count, 2 * quarter, 2 * quarter, channels)


def split_heads(groups, w_qkv):
    count, rows_all, _ = groups.shape
    triple = jnp.dot(groups, w_qkv, preferred_element_type=jnp.float32).astype(jnp.bfloat16)
    triple = triple.reshape(count, rows_all, 3, HEADS, HEAD_DIM)
    return (triple[:, :, 0], triple[:, :, 1], triple[:, :, 2])


def score(queries, key_rows):
    return jnp.einsum(
        "iqhe,ikhe->ihqk", queries, key_rows, preferred_element_type=jnp.float32
    ) * HEAD_DIM ** (-0.5)


def shards(
    tokens, condition, counts, w_mod, w_qkv, w_out, w_up, w_down, conv_attn, conv_ffn, cotangent
):
    item_count, _, quad_rows, channels = tokens.shape
    half_side = math.isqrt(quad_rows)
    corner = lax.axis_index("narrow")
    row_half = corner // 2
    col_half = corner % 2
    living = (jnp.arange(item_count, dtype=jnp.int32) < counts[0]).astype(jnp.float32)[
        :, None, None, None
    ]
    start_map = tokens.reshape(item_count, half_side, half_side, channels).astype(jnp.float32)
    cond_f = condition.astype(jnp.float32)
    lifted = jax.nn.silu(cond_f).astype(jnp.bfloat16)
    modulation = jnp.dot(lifted, w_mod, preferred_element_type=jnp.float32).reshape(
        item_count, 6, channels
    )
    pieces = [modulation[:, place][:, None, None, :] for place in range(6)]
    shift_a, scale_a, gate_a, shift_f, scale_f, gate_f = pieces
    first_f, pull_attn_norm = jax.vjp(modulate, start_map, shift_a, scale_a)
    first_in = first_f.astype(jnp.bfloat16)
    padded_attn = extend(first_in, row_half, col_half, attn_across, attn_down)
    mixed_map = apply_taps(padded_attn, conv_attn, half_side, False).astype(jnp.bfloat16)
    groups = to_groups(mixed_map)
    queries, key_rows, values = split_heads(groups, w_qkv)
    scores = score(queries, key_rows)
    peak = jnp.max(scores, -1, keepdims=True)
    raised_exp = jnp.exp(scores - peak)
    summed = jnp.sum(raised_exp, -1, keepdims=True)
    attn_probs = (raised_exp / summed).astype(jnp.bfloat16)
    log_total = peak + jnp.log(summed)
    attended = jnp.einsum("ihqk,ikhe->iqhe", attn_probs, values, preferred_element_type=jnp.float32)
    attended = attended.astype(jnp.bfloat16).reshape(item_count, quad_rows, channels)
    returned = to_quads(attended)
    branch = jnp.dot(returned, w_out, preferred_element_type=jnp.float32)
    hidden_one = start_map + gate_a * branch
    second_f, pull_ffn_norm = jax.vjp(modulate, hidden_one, shift_f, scale_f)
    second = second_f.astype(jnp.bfloat16)
    raised = jnp.dot(second, w_up, preferred_element_type=jnp.float32).astype(jnp.bfloat16)
    padded_ffn = extend(raised, row_half, col_half, ffn_across, ffn_down)
    filtered = apply_taps(padded_ffn, conv_ffn, half_side, False)
    activated = gelu_tanh(filtered).astype(jnp.bfloat16)
    branch_two = jnp.dot(activated, w_down, preferred_element_type=jnp.float32)
    output = ((hidden_one + gate_f * branch_two) * living).astype(jnp.bfloat16)
    grad_res = (
        cotangent.reshape(item_count, half_side, half_side, channels).astype(jnp.float32) * living
    )
    d_gate_f = jnp.sum(grad_res * branch_two, (1, 2))
    d_branch_two = (grad_res * gate_f).astype(jnp.bfloat16)
    down_grad = jnp.einsum(
        "ixyf,ixyd->fd", activated, d_branch_two, preferred_element_type=jnp.float32
    )
    d_activated = jnp.einsum(
        "ixyd,fd->ixyf", d_branch_two, w_down, preferred_element_type=jnp.float32
    )
    again = jnp.dot(second, w_up, preferred_element_type=jnp.float32).astype(jnp.bfloat16)
    kept_pad = extend(again, row_half, col_half, ffn_across, ffn_down)
    kept_filter = apply_taps(kept_pad, conv_ffn, half_side, False)
    _, gelu_pull = jax.vjp(gelu_tanh, kept_filter)
    d_filtered = gelu_pull(d_activated)[0].astype(jnp.bfloat16)
    conv_ffn_grad = tap_grads(kept_pad, d_filtered, half_side)
    d_padded_ffn = extend(d_filtered, row_half, col_half, ffn_across, ffn_down)
    d_raised = apply_taps(d_padded_ffn, conv_ffn, half_side, True).astype(jnp.bfloat16)
    up_grad = jnp.einsum("ixyd,ixyf->df", second, d_raised, preferred_element_type=jnp.float32)
    d_second = jnp.einsum("ixyf,df->ixyd", d_raised, w_up, preferred_element_type=jnp.float32)
    d_hidden_part, d_shift_f, d_scale_f = pull_ffn_norm(d_second)
    d_hidden = grad_res + d_hidden_part
    d_gate_a = jnp.sum(d_hidden * branch, (1, 2))
    d_branch = (d_hidden * gate_a).astype(jnp.bfloat16)
    proj_grad = jnp.einsum("ixyd,ixye->de", returned, d_branch, preferred_element_type=jnp.float32)
    d_returned = jnp.einsum(
        "ixye,de->ixyd", d_branch, w_out, preferred_element_type=jnp.float32
    ).astype(jnp.bfloat16)
    d_attended = to_groups(d_returned).reshape(item_count, quad_rows, HEADS, HEAD_DIM)
    queries, key_rows, values = split_heads(groups, w_qkv)
    scores = score(queries, key_rows)
    exact = jnp.exp(scores - log_total)
    rounded = exact.astype(jnp.bfloat16)
    d_probs = jnp.einsum("iqhe,ikhe->ihqk", d_attended, values, preferred_element_type=jnp.float32)
    d_values = jnp.einsum(
        "ihqk,iqhe->ikhe", rounded, d_attended, preferred_element_type=jnp.float32
    )
    d_scores = (exact * (d_probs - jnp.sum(d_probs * exact, -1, keepdims=True))).astype(
        jnp.bfloat16
    )
    d_queries = jnp.einsum(
        "ihqk,ikhe->iqhe", d_scores, key_rows, preferred_element_type=jnp.float32
    ) * HEAD_DIM ** (-0.5)
    d_keys = jnp.einsum(
        "ihqk,iqhe->ikhe", d_scores, queries, preferred_element_type=jnp.float32
    ) * HEAD_DIM ** (-0.5)
    d_triple = (
        jnp.stack([d_queries, d_keys, d_values], 2)
        .astype(jnp.bfloat16)
        .reshape(item_count, quad_rows, 3 * channels)
    )
    qkv_grad = jnp.einsum("iqd,iqe->de", groups, d_triple, preferred_element_type=jnp.float32)
    d_groups = jnp.einsum(
        "iqe,de->iqd", d_triple, w_qkv, preferred_element_type=jnp.float32
    ).astype(jnp.bfloat16)
    d_mixed = to_quads(d_groups)
    conv_attn_grad = tap_grads(padded_attn, d_mixed, half_side)
    d_padded_attn = extend(d_mixed, row_half, col_half, attn_across, attn_down)
    d_first = apply_taps(d_padded_attn, conv_attn, half_side, True).astype(jnp.bfloat16)
    d_start, d_shift_a, d_scale_a = pull_attn_norm(d_first.astype(jnp.float32))
    token_grad = (d_hidden + d_start).astype(jnp.bfloat16).reshape(tokens.shape)
    flat_parts = [
        d_shift_a.reshape(item_count, channels),
        d_scale_a.reshape(item_count, channels),
        d_gate_a,
        d_shift_f.reshape(item_count, channels),
        d_scale_f.reshape(item_count, channels),
        d_gate_f,
    ]
    d_modulation = jnp.stack(flat_parts, 1).reshape(item_count, 6 * channels)
    _, silu_pull = jax.vjp(jax.nn.silu, cond_f)
    w_mod_f = w_mod.astype(jnp.float32)
    mod_grad = jnp.einsum(
        "id,im->dm", lifted.astype(jnp.float32), d_modulation, precision=lax.Precision.HIGHEST
    )
    d_lifted = jnp.einsum("im,dm->id", d_modulation, w_mod_f, precision=lax.Precision.HIGHEST)
    cond_part = silu_pull(d_lifted)[0]
    cond_grad = lax.psum(cond_part, "narrow")
    mod_sum = lax.psum_scatter(mod_grad, ("wide", "narrow"), scatter_dimension=0, tiled=True)
    qkv_sum, proj_sum, up_sum, down_sum, conv_attn_sum, conv_ffn_sum = (
        lax.psum_scatter(qkv_grad, ("wide", "narrow"), scatter_dimension=0, tiled=True),
        lax.psum_scatter(proj_grad, ("wide", "narrow"), scatter_dimension=0, tiled=True),
        lax.psum_scatter(up_grad, ("wide", "narrow"), scatter_dimension=0, tiled=True),
        lax.psum_scatter(down_grad, ("wide", "narrow"), scatter_dimension=0, tiled=True),
        lax.psum_scatter(conv_attn_grad, ("wide", "narrow"), scatter_dimension=0, tiled=True),
        lax.psum_scatter(conv_ffn_grad, ("wide", "narrow"), scatter_dimension=0, tiled=True),
    )
    return (
        output.reshape(tokens.shape),
        token_grad,
        cond_grad,
        mod_sum,
        qkv_sum,
        proj_sum,
        up_sum,
        down_sum,
        conv_attn_sum,
        conv_ffn_sum,
    )


def solution(mesh):
    in_specs = (
        P("wide", "narrow", None, None),
        P("wide", None),
        P("wide"),
        P(),
        P(),
        P(),
        P(),
        P(),
        P(),
        P(),
        P("wide", "narrow", None, None),
    )
    out_specs = (
        P("wide", "narrow", None, None),
        P("wide", "narrow", None, None),
        P("wide", None),
        P(("wide", "narrow"), None),
        P(("wide", "narrow"), None),
        P(("wide", "narrow"), None),
        P(("wide", "narrow"), None),
        P(("wide", "narrow"), None),
        P(("wide", "narrow"), None),
        P(("wide", "narrow"), None),
    )
    return jax.shard_map(shards, mesh=mesh, in_specs=in_specs, out_specs=out_specs, check_vma=False)
```

profile of v0, /device:TPU:0, one launch (start us, length us, event | category | flops | bytes accessed | tf_op | source)
XLA Modules:
  0.0 1023.2 jit_solution(16470884249242052527)
XLA Ops:
  52.8 18.9 %all_to_all.20 = bf16[3,4,64,768]{3,2,0,1:T(8,128)(2,1)S(1)} all-to-all(bf16[3,4,64,768]{3,2,0,1:T(8,128)(2,1)S(1)} %bitcast.210), channel_id=1, replica_groups=mesh['wide'=8,'narrow'=4] {'narrow'}, dimensions={1} | all-to-all | bytes 2359296 | tf_op jit(solution)/shard_map/all_to_all | solution.py:99
  77.2 5.7 copy.78
  99.5 5.1 copy.83
  110.8 14.0 %all-to-all-done.1 = bf16[3,4,64,768]{3,2,0,1:T(8,128)(2,1)} async-done(((bf16[3,4,64,768]{3,2,0,1:T(8,128)(2,1)}), bf16[3,4,64,768]{3,2,0,1:T(8,128)(2,1)}, u32[]{:S(2)}, u32[]{:S(2)}) %all-to-all-start.1) | async-done | bytes 1179680 | tf_op jit(solution)/shard_map/all_to_all | solution.py:106
  132.0 5.0 fusion.118
  147.9 10.8 %collective-permute-done.3 = bf16[3,1,18,3072]{3,2,1,0:T(8,128)(2,1)S(1)} collective-permute-done((bf16[3,1,18,3072]{3,2,1,0:T(8,128)(2,1)S(1)}, bf16[3,1,18,3072]{3,2,1,0:T(8,128)(2,1)S(1)}, u32[]{:S(2)}, u32[]{:S(2)}) %collective-permute-start.3) | collective-permute-done | bytes 331808 | tf_op jit(solution)/shard_map/ppermute | solution.py:16
  158.8 10.2 maximum_maximum_fusion
  169.1 15.6 %fusion.7 = f32[3,16,16,3072]{3,2,1,0:T(8,128)} fusion(bf16[3,16,16,3072]{3,2,1,0:T(8,128)(2,1)S(1)} %convolution_convert_fusion.1, bf16[3,16,1,3072]{3,2,1,0:T(2,128)(2,1)} %copy-done.23, bf16[3,16,1,3072]{3,2,1,0:T(2,128)(2,1)S(1)} %get-tuple-element.117, f32[3072]{0:T(1024)S(1)} %bitcast.235, f32[3072]{0:T(1024)S(1)} %bitcast.233, f32[3072]{0:T(1024)S(1)} %bitcast.231, ...), kind=kLoop, calls=%fused_computation.28 | loop fusion | flops 75497472 | bytes 43167744 | tf_op jit(solution)/shard_map/add | solution.py:77
  184.8 35.4 %fusion.29 = (f32[3072]{0:T(1024)}, f32[3072]{0:T(1024)}, f32[3072]{0:T(1024)}, f32[3072]{0:T(1024)}, f32[3072]{0:T(1024)}, /*index=5*/f32[3072]{0:T(1024)}, f32...) fusion(bf16[3,17,18,3072]{3,2,1,0:T(8,128)(2,1)} %copy-done.4, ...), kind=kOutput, calls=%fused_computation.50 | convolution fusion | flops 3753612288 | bytes 53793804 | tf_op jit(solution)/shard_map/ixyd,fd->ixyf/dot_general | solution.py:177
  235.4 5.9 collective-permute-done.5
  242.5 12.8 %pad_maximum_fusion.1 = (bf16[3,17,18,3072]{3,2,1,0:T(8,128)(2,1)S(1)}, bf16[3,17,18,3072]{3,2,1,0:T(8,128)(2,1)S(1)}) fusion(bf16[3,1,18,3072]{3,2,1,0:T(8,128)(2,1)S(1)} %get-tuple-element.111, bf16[3,16,1,3072]{3,2,1,0:T(2,128)(2,1)} %copy-done.21, bf16[3,16,16,3072]{3,2,1,0:T(8,128)(2,1)} %get-tuple-element.151, bf16[3,16,1,3072]{3,2,1,0:T(2,128)(2,1)} %copy-done.19, ...), kind=kLoop, calls=%fused_computation.61 | loop fusion | flops 45121536 | bytes 17252352 | tf_op jit(solution)/shard_map/concatenate | solution.py:62
  255.5 15.6 %fusion.20 = bf16[3,16,16,3072]{3,2,1,0:T(8,128)(2,1)} fusion(bf16[3,16,16,3072]{3,2,1,0:T(8,128)(2,1)S(1)} %bitcast.200, bf16[3,17,18,3072]{3,2,1,0:T(8,128)(2,1)S(1)} %get-tuple-element.100, bf16[3,16,1,3072]{3,2,1,0:T(2,128)(2,1)S(1)} %copy-done.20, bf16[3,16,1,3072]{3,2,1,0:T(2,128)(2,1)} %copy-done.21, ...), kind=kLoop, calls=%fused_computation.41 | loop fusion | flops 77856768 | bytes 38449152 | tf_op jit(solution)/shard_map/convert_element_type | solution.py:187
  271.1 8.7 multiply_reduce_fusion.5
  281.9 11.9 %fusion.80 = (f32[3,768]{1,0:T(4,128)}, bf16[3,16,16,768]{3,2,1,0:T(8,128)(2,1)}, f32[3,768]{1,0:T(4,128)}, f32[3,16,16,768]{3,2,1,0:T(8,128)S(1)}) fusion(bf16[3,16,16,768]{3,2,1,0:T(8,128)(2,1)S(1)} %bitcast.250, f32[3]{0:T(128)S(1)} %compare_convert_fusion, f32[3,16,16,768]{3,2,1,0:T(8,128)S(1)} %copy-done.10, f32[3,768]{1,0:T(4,128)S(1)} %copy-done.104, ...), kind=kOutput, calls=%fused_computation.142 | convolution fusion | flops 3655724544 | bytes 26001420 | tf_op jit(solution)/shard_map/dot_general | solution.py:167
  312.4 11.2 %all-to-all-done.2 = bf16[3,4,64,768]{3,2,0,1:T(8,128)(2,1)} async-done(((bf16[3,4,64,768]{3,2,0,1:T(8,128)(2,1)}), bf16[3,4,64,768]{3,2,0,1:T(8,128)(2,1)}, u32[]{:S(2)}, u32[]{:S(2)}) %all-to-all-start.2) | async-done | bytes 1179680 | tf_op jit(solution)/shard_map/all_to_all | solution.py:99
  323.6 5.3 copy.94
  333.4 10.9 %multiply_reduce_fusion = (f32[3,12,256]{2,1,0:T(8,128)}, f32[3,12,256,256]{2,3,1,0:T(8,128)}) fusion(f32[3,12,256,256]{2,3,1,0:T(8,128)} %copy-done.1, f32[3,12,256]{2,1,0:T(8,128)} %log_add_fusion, bf16[3,256,12,64]{1,3,2,0:T(8,128)(2,1)} %reshape_reshape.7, bf16[3,256,3,12,64]{1,4,3,2,0:T(8,128)(2,1)} %bitcast.203), kind=kOutput, calls=%fused_computation.52 | convolution fusion | flops 311417856 | bytes 21319680 | tf_op jit(solution)/shard_map/iqhe,ikhe->ihqk/dot_general | solution.py:203
  344.4 11.6 %multiply_convert_fusion = bf16[3,12,256,256]{2,3,1,0:T(8,128)(2,1)} fusion(f32[3,12,256,256]{2,3,1,0:T(8,128)} %get-tuple-element.150, f32[3,12,256,256]{2,3,1,0:T(8,128)} %copy-done.1, f32[3,12,256]{2,1,0:T(8,128)} %get-tuple-element.149, f32[3,12,256]{2,1,0:T(8,128)} %log_add_fusion), kind=kLoop, calls=%fused_computation.51 | loop fusion | flops 11796480 | bytes 23666688 | tf_op jit(solution)/shard_map/convert_element_type | solution.py:207
  362.8 5.6 fusion.81
  371.1 5.0 convolution_bitcast_fusion.2
  376.8 13.3 %convolution_bitcast_fusion = f32[3072,768]{1,0:T(8,128)} fusion(bf16[3,16,16,768]{3,2,1,0:T(8,128)(2,1)} %bitcast.249, f32[3]{0:T(128)S(1)} %compare_convert_fusion, f32[3,768]{1,0:T(4,128)S(1)} %copy-done.105, f32[3,16,16,3072]{3,2,1,0:T(8,128)} %fusion.7), kind=kOutput, calls=%fused_computation.74 | convolution fusion | flops 3647471616 | bytes 20063244 | tf_op jit(solution)/shard_map/ixyf,ixyd->fd/dot_general | solution.py:174
  390.8 10.8 %convolution_bitcast_fusion.1 = f32[768,3072]{1,0:T(8,128)} fusion(bf16[3,16,16,3072]{3,2,1,0:T(8,128)(2,1)} %fusion.20, f32[3,16,16,768]{3,2,1,0:T(8,128)} %copy-done.9, f32[3,768]{1,0:T(4,128)} %get-tuple-element.152, f32[3,768]{1,0:T(4,128)S(1)} %copy-done.72, f32[3,16,16]{2,1,0:T(8,128)} %copy-done.31, f32[3,16,16]{2,1,0:T(8,128)} %copy-done.29), kind=kOutput, calls=%fused_computation.75 | convolution fusion | flops 3626827776 | bytes 16539648 | tf_op jit(solution)/shard_map/ixyd,ixyf->df/dot_general | solution.py:188
  406.7 18.7 %all_to_all.21 = bf16[3,4,64,768]{3,2,0,1:T(8,128)(2,1)S(1)} all-to-all(bf16[3,4,64,768]{3,2,0,1:T(8,128)(2,1)S(1)} %copy.100), channel_id=1, replica_groups=mesh['wide'=8,'narrow'=4] {'narrow'}, dimensions={1} | all-to-all | bytes 2359296 | tf_op jit(solution)/shard_map/all_to_all | solution.py:106
  451.6 8.9 fusion.112
  462.0 8.1 fusion.75
  487.2 41.9 %all-reduce = f32[768,9]{0,1:T(8,128)} all-reduce(f32[768,9]{0,1:T(8,128)} %stack.97), channel_id=7, replica_groups=mesh['wide'=8,'narrow'=4] {'wide','narrow'}, use_global_device_ids=true, to_apply=%region_32.33.clone | all-reduce | flops 6912 | bytes 55296
  530.5 9.2 fusion.108
  539.6 12.6 %psum.7 = f32[3,768]{1,0:T(4,128)} all-reduce(f32[3,768]{1,0:T(4,128)} %fusion.108), channel_id=1, replica_groups=mesh['wide'=8,'narrow'=4] {'narrow'}, use_global_device_ids=true, to_apply=%region_17.18 | all-reduce | flops 2304 | bytes 18432 | tf_op jit(solution)/shard_map/psum | solution.py:247
  557.0 7.8 reduce-scatter.12.cloned.1.call-done
  564.8 141.5 %reduce-scatter.18.cloned.1.call-done = f32[96,768]{1,0:T(8,128)} async-done(((f32[3072,768]{1,0:T(8,128)}), f32[96,768]{1,0:T(8,128)}) %reduce-scatter.18.cloned.1.call-update) | async-done | bytes 294928 | tf_op jit(solution)/shard_map/reduce_scatter | solution.py:253
  706.3 141.5 %reduce-scatter.16.cloned.1.call-done = f32[24,3072]{1,0:T(8,128)} async-done(((f32[768,3072]{1,0:T(8,128)}), f32[24,3072]{1,0:T(8,128)}) %reduce-scatter.16.cloned.1.call-update) | async-done | bytes 294928 | tf_op jit(solution)/shard_map/reduce_scatter | solution.py:252
  847.8 168.4 %reduce-scatter.10.cloned.1.call-done = f32[24,4608]{1,0:T(8,128)} async-done(((f32[768,4608]{1,0:T(8,128)}), f32[24,4608]{1,0:T(8,128)}) %reduce-scatter.10.cloned.1.call-update) | async-done | bytes 442384 | tf_op jit(solution)/shard_map/reduce_scatter | solution.py:248
  (354 shorter events, 198.7 us)
Async XLA Ops:
  7.2 65.7 %copy-start = (bf16[768,2304]{1,0:T(8,128)(2,1)S(1)}, bf16[768,2304]{1,0:T(8,128)(2,1)}, u32[]{:S(2)}) copy-start(bf16[768,2304]{1,0:T(8,128)(2,1)} %param.15) | copy-start | bytes 10616836
  28.7 1.8 collective-permute-start
  32.8 6.3 collective-permute-start.1
  104.6 20.2 %all-to-all-start.1 = ((bf16[3,4,64,768]{3,2,0,1:T(8,128)(2,1)}), bf16[3,4,64,768]{3,2,0,1:T(8,128)(2,1)}, u32[]{:S(2)}, u32[]{:S(2)}) async-start(bf16[3,4,64,768]{3,2,0,1:T(8,128)(2,1)} %copy.83), calls=%async_computation.1 | async-start | bytes 2359296 | tf_op jit(solution)/shard_map/all_to_all | solution.py:106
  108.9 351.6 %reduce-scatter.20.cloned.1.call-start = ((), (), s32[]{:S(2)}) async-start(), calls=%async_computation.15 | async-start | bytes 1622016
  142.3 26.7 %copy-start.5 = (bf16[3,16,16,3072]{3,2,1,0:T(8,128)(2,1)}, bf16[3,16,16,3072]{3,2,1,0:T(8,128)(2,1)S(1)}, u32[]{:S(2)}) copy-start(bf16[3,16,16,3072]{3,2,1,0:T(8,128)(2,1)S(1)} %convolution_convert_fusion.1) | copy-start | bytes 14155780
  143.4 1.6 collective-permute-start.2
  146.0 23.0 %copy-start.22 = (bf16[3,16,1,3072]{3,2,1,0:T(2,128)(2,1)}, bf16[3,16,1,3072]{3,2,1,0:T(2,128)(2,1)S(1)}, u32[]{:S(2)}) copy-start(bf16[3,16,1,3072]{3,2,1,0:T(2,128)(2,1)S(1)} %get-tuple-element.117) | copy-start | bytes 884740
  146.4 12.3 %collective-permute-start.3 = (bf16[3,1,18,3072]{3,2,1,0:T(8,128)(2,1)S(1)}, bf16[3,1,18,3072]{3,2,1,0:T(8,128)(2,1)S(1)}, u32[]{:S(2)}, u32[]{:S(2)}) collective-permute-start(bf16[3,1,18,3072]{3,2,1,0:T(8,128)(2,1)S(1)} %fusion.96), channel_id=1, source_target_pairs={{0,2},{1,3},{2,0},{3,1},{4,6},{5,7},{6,4},{7,5},{8,10},{9,11},{10,... | collective-permute-start | bytes 995336 | tf_op jit(solution)/shard_map/ppermute | solution.py:16
  147.1 21.9 %copy-start.51 = (f32[3072,1]{0,1:T(1,128)}, f32[3072,1]{0,1:T(1,128)S(1)}, u32[]{:S(2)}) copy-start(f32[3072,1]{0,1:T(1,128)S(1)} %get-tuple-element.127) | copy-start | bytes 36868
  147.1 21.9 %copy-start.53 = (f32[3072,1]{0,1:T(1,128)}, f32[3072,1]{0,1:T(1,128)S(1)}, u32[]{:S(2)}) copy-start(f32[3072,1]{0,1:T(1,128)S(1)} %get-tuple-element.128) | copy-start | bytes 36868
  147.1 21.9 %copy-start.55 = (f32[3072,1]{0,1:T(1,128)}, f32[3072,1]{0,1:T(1,128)S(1)}, u32[]{:S(2)}) copy-start(f32[3072,1]{0,1:T(1,128)S(1)} %get-tuple-element.129) | copy-start | bytes 36868
  147.2 21.9 %copy-start.57 = (f32[3072,1]{0,1:T(1,128)}, f32[3072,1]{0,1:T(1,128)S(1)}, u32[]{:S(2)}) copy-start(f32[3072,1]{0,1:T(1,128)S(1)} %get-tuple-element.130) | copy-start | bytes 36868
  147.2 21.9 %copy-start.59 = (f32[3072,1]{0,1:T(1,128)}, f32[3072,1]{0,1:T(1,128)S(1)}, u32[]{:S(2)}) copy-start(f32[3072,1]{0,1:T(1,128)S(1)} %get-tuple-element.131) | copy-start | bytes 36868
  147.2 21.9 %copy-start.61 = (f32[3072,1]{0,1:T(1,128)}, f32[3072,1]{0,1:T(1,128)S(1)}, u32[]{:S(2)}) copy-start(f32[3072,1]{0,1:T(1,128)S(1)} %get-tuple-element.132) | copy-start | bytes 36868
  147.2 21.9 %copy-start.63 = (f32[3072,1]{0,1:T(1,128)}, f32[3072,1]{0,1:T(1,128)S(1)}, u32[]{:S(2)}) copy-start(f32[3072,1]{0,1:T(1,128)S(1)} %get-tuple-element.133) | copy-start | bytes 36868
  147.2 21.9 %copy-start.65 = (f32[3072,1]{0,1:T(1,128)}, f32[3072,1]{0,1:T(1,128)S(1)}, u32[]{:S(2)}) copy-start(f32[3072,1]{0,1:T(1,128)S(1)} %get-tuple-element.134) | copy-start | bytes 36868
  147.2 21.9 %copy-start.67 = (f32[3072,1]{0,1:T(1,128)}, f32[3072,1]{0,1:T(1,128)S(1)}, u32[]{:S(2)}) copy-start(f32[3072,1]{0,1:T(1,128)S(1)} %get-tuple-element.135) | copy-start | bytes 36868
  169.0 15.8 %copy-start.3 = (bf16[3,17,18,3072]{3,2,1,0:T(8,128)(2,1)}, bf16[3,17,18,3072]{3,2,1,0:T(8,128)(2,1)S(1)}, u32[]{:S(2)}) copy-start(bf16[3,17,18,3072]{3,2,1,0:T(8,128)(2,1)S(1)} %get-tuple-element.101) | copy-start | bytes 16920580
  169.0 15.8 %copy-start.4 = (bf16[3,17,18,3072]{3,2,1,0:T(8,128)(2,1)}, bf16[3,17,18,3072]{3,2,1,0:T(8,128)(2,1)S(1)}, u32[]{:S(2)}) copy-start(bf16[3,17,18,3072]{3,2,1,0:T(8,128)(2,1)S(1)} %get-tuple-element.102) | copy-start | bytes 16920580
  223.5 1.6 collective-permute-start.4
  228.8 12.5 %collective-permute-start.5 = (bf16[3,1,18,3072]{3,2,1,0:T(8,128)(2,1)}, bf16[3,1,18,3072]{3,2,1,0:T(8,128)(2,1)}, u32[]{:S(2)}, u32[]{:S(2)}) collective-permute-start(bf16[3,1,18,3072]{3,2,1,0:T(8,128)(2,1)} %fusion.95), channel_id=1, source_target_pairs={{0,2},{1,3},{2,0},{3,1},{4,6},{5,7},{6,4},{7,5},{8,10},{9,11},{10,... | collective-permute-start | bytes 995336 | tf_op jit(solution)/shard_map/ppermute | solution.py:16
  255.5 15.6 %copy-start.30 = (f32[3,16,16]{2,1,0:T(8,128)S(1)}, f32[3,16,16]{2,1,0:T(8,128)}, u32[]{:S(2)}) copy-start(f32[3,16,16]{2,1,0:T(8,128)} %copy-done.29) | copy-start | bytes 9220
  255.5 15.6 %copy-start.71 = (f32[3,768]{1,0:T(4,128)S(1)}, f32[3,768]{1,0:T(4,128)}, u32[]{:S(2)}) copy-start(f32[3,768]{1,0:T(4,128)} %get-tuple-element.153) | copy-start | bytes 27652
  303.4 20.2 %all-to-all-start.2 = ((bf16[3,4,64,768]{3,2,0,1:T(8,128)(2,1)}), bf16[3,4,64,768]{3,2,0,1:T(8,128)(2,1)}, u32[]{:S(2)}, u32[]{:S(2)}) async-start(bf16[3,4,64,768]{3,2,0,1:T(8,128)(2,1)} %bitcast.208), calls=%async_computation.2 | async-start | bytes 2359296 | tf_op jit(solution)/shard_map/all_to_all | solution.py:99
  307.7 249.3 %reduce-scatter.14.cloned.1.call-start = ((), (), s32[]{:S(2)}) async-start(), calls=%async_computation.12 | async-start | bytes 2433024 | tf_op jit(solution)/shard_map/reduce_scatter | solution.py:251
  312.3 252.5 %reduce-scatter.12.cloned.1.call-start = ((), (), s32[]{:S(2)}) async-start(), calls=%async_computation.11 | async-start | bytes 7299072 | tf_op jit(solution)/shard_map/reduce_scatter | solution.py:250
  376.1 330.2 %reduce-scatter.18.cloned.1.call-start = ((), (), s32[]{:S(2)}) async-start(), calls=%async_computation.14 | async-start | bytes 9732096 | tf_op jit(solution)/shard_map/reduce_scatter | solution.py:253
  390.1 457.7 %reduce-scatter.16.cloned.1.call-start = ((), (), s32[]{:S(2)}) async-start(), calls=%async_computation.13 | async-start | bytes 9732096 | tf_op jit(solution)/shard_map/reduce_scatter | solution.py:252
  401.6 614.5 %reduce-scatter.10.cloned.1.call-start = ((), (), s32[]{:S(2)}) async-start(), calls=%async_computation.10 | async-start | bytes 14598144 | tf_op jit(solution)/shard_map/reduce_scatter | solution.py:248
  433.9 1.4 collective-permute-start.6
  436.7 5.2 collective-permute-start.7
  (95 other events, 488.1 us)
Sparse Core Ops, SparseCore 0:
  235.5 99.2 reduce-scatter.19
  340.7 98.6 reduce-scatter.13
  445.7 119.0 reduce-scatter.11
  571.1 135.1 reduce-scatter.17
  712.6 135.1 reduce-scatter.15
  854.2 161.8 reduce-scatter.9
where the time goes:
time: 1030 us; the launch traced here: 1020 us
  waiting for transfers between devices  514 us (50%)
  matrix products  164 us (16%)
  other arithmetic  128 us (12%)
  local copies, waits for them, and re-layouts  94.3 us (9%)
  blocking collectives  92.1 us (9%)
  between operations  16.6 us (2%)
  starting transfers between devices  14.5 us (1%)
    reduce_scatter x1, waiting for transfers between devices, shards(): lax.psum_scatter(mod_grad, ('wide', 'narrow'), scatter_dimension=0, tiled...  168 us
    reduce_scatter x1, waiting for transfers between devices, shards(): lax.psum_scatter(up_grad, ('wide', 'narrow'), scatter_dimension=0, tiled=...  141 us
    reduce_scatter x1, waiting for transfers between devices, shards(): lax.psum_scatter(down_grad, ('wide', 'narrow'), scatter_dimension=0, tile...  141 us
    unnamed x1, blocking collectives  41.9 us
    dot_general x1, matrix products, shards(): jnp.einsum('ixyd,fd->ixyf', d_branch_two, w_down, preferred_element_type=...  35.4 us
    ppermute x8, waiting for transfers between devices, from_partner(): lax.ppermute(shard, axis, [(i, i ^ 1 << bit) for i in range(lax.axis_size...  29.7 us
    concatenate x4, other arithmetic, extend(): return jnp.concatenate([top_rim, widened, bottom_rim], 1)  28.1 us
    unnamed x233, local copies, waits for them, and re-layouts  22.2 us
  transfers between devices with their start and end apart: 16, of which 14 were waited for; matrix products, arithmetic and copies ran while one was open for 22% of the time, Pallas kernels for 0%

commit v1 on v0

--- a/solution.py
+++ b/solution.py
@@ -122,6 +122,56 @@
     ) * HEAD_DIM ** (-0.5)
 
 
+def narrow_sum(part):
+    for bit in range(lax.axis_size("narrow").bit_length() - 1):
+        part = part + from_partner(part, "narrow", bit)
+    return part
+
+
+def wide_gather(block):
+    count = lax.axis_size("wide")
+    place = lax.axis_index("wide")
+    held = block[None]
+    for bit in range(count.bit_length() - 1):
+        other = from_partner(held, "wide", bit)
+        mine_high = (place >> bit) & 1
+        low = jnp.where(mine_high == 1, other, held)
+        high = jnp.where(mine_high == 1, held, other)
+        held = jnp.concatenate([low, high], 0)
+    return held.reshape((count * block.shape[0],) + block.shape[1:])
+
+
+def split_dot(exact, coarse, dims):
+    high = exact.astype(jnp.bfloat16)
+    low = (exact - high.astype(jnp.float32)).astype(jnp.bfloat16)
+    high_dot = lax.dot_general(high, coarse, (dims, ((), ())), preferred_element_type=jnp.float32)
+    low_dot = lax.dot_general(low, coarse, (dims, ((), ())), preferred_element_type=jnp.float32)
+    return high_dot + low_dot
+
+
+def halving_sum(blocks, colour):
+    wide_bits = lax.axis_size("wide").bit_length() - 1
+    narrow_bits = lax.axis_size("narrow").bit_length() - 1
+    order = [("narrow", 0)]
+    first = [("wide", 0), ("narrow", 1)]
+    order += first if colour == 0 else first[::-1]
+    order += [("wide", bit) for bit in range(1, wide_bits)]
+    names = [("wide", bit) for bit in range(wide_bits - 1, -1, -1)]
+    names += [("narrow", bit) for bit in range(narrow_bits - 1, -1, -1)]
+    held = blocks.reshape((2,) * len(names) + blocks.shape[1:])
+    for step, (axis, bit) in enumerate(order):
+        where = names.index((axis, bit))
+        names.pop(where)
+        mine = (lax.axis_index(axis) >> bit) & 1
+        keep = lax.dynamic_index_in_dim(held, mine, where, keepdims=False)
+        give = lax.dynamic_index_in_dim(held, 1 - mine, where, keepdims=False)
+        got = from_partner(give, axis, bit)
+        held = keep.astype(jnp.float32) + got.astype(jnp.float32)
+        if step < len(order) - 1:
+            held = held.astype(jnp.bfloat16)
+    return held
+
+
 def shards(
     tokens, condition, counts, w_mod, w_qkv, w_out, w_up, w_down, conv_attn, conv_ffn, cotangent
 ):
@@ -136,6 +186,7 @@
     start_map = tokens.reshape(item_count, half_side, half_side, channels).astype(jnp.float32)
     cond_f = condition.astype(jnp.float32)
     lifted = jax.nn.silu(cond_f).astype(jnp.bfloat16)
+    all_lifted = wide_gather(lifted)
     modulation = jnp.dot(lifted, w_mod, preferred_element_type=jnp.float32).reshape(
         item_count, 6, channels
     )
@@ -237,23 +288,37 @@
         d_gate_f,
     ]
     d_modulation = jnp.stack(flat_parts, 1).reshape(item_count, 6 * channels)
+    d_modulation = narrow_sum(d_modulation)
     _, silu_pull = jax.vjp(jax.nn.silu, cond_f)
-    w_mod_f = w_mod.astype(jnp.float32)
-    mod_grad = jnp.einsum(
-        "id,im->dm", lifted.astype(jnp.float32), d_modulation, precision=lax.Precision.HIGHEST
-    )
-    d_lifted = jnp.einsum("im,dm->id", d_modulation, w_mod_f, precision=lax.Precision.HIGHEST)
-    cond_part = silu_pull(d_lifted)[0]
-    cond_grad = lax.psum(cond_part, "narrow")
-    mod_sum = lax.psum_scatter(mod_grad, ("wide", "narrow"), scatter_dimension=0, tiled=True)
-    qkv_sum, proj_sum, up_sum, down_sum, conv_attn_sum, conv_ffn_sum = (
-        lax.psum_scatter(qkv_grad, ("wide", "narrow"), scatter_dimension=0, tiled=True),
-        lax.psum_scatter(proj_grad, ("wide", "narrow"), scatter_dimension=0, tiled=True),
-        lax.psum_scatter(up_grad, ("wide", "narrow"), scatter_dimension=0, tiled=True),
-        lax.psum_scatter(down_grad, ("wide", "narrow"), scatter_dimension=0, tiled=True),
-        lax.psum_scatter(conv_attn_grad, ("wide", "narrow"), scatter_dimension=0, tiled=True),
-        lax.psum_scatter(conv_ffn_grad, ("wide", "narrow"), scatter_dimension=0, tiled=True),
-    )
+    d_lifted = split_dot(d_modulation, w_mod, ((1,), (1,)))
+    cond_grad = silu_pull(d_lifted)[0]
+    all_modulation = wide_gather(d_modulation)
+    block_rows = channels // (lax.axis_size("wide") * lax.axis_size("narrow"))
+    own_block = lax.axis_index("wide") * lax.axis_size("narrow") + corner
+    own_lifted = lax.dynamic_slice_in_dim(all_lifted, own_block * block_rows, block_rows, 1)
+    mod_sum = split_dot(all_modulation, own_lifted, ((0,), (0,))).T
+    blocks = lax.axis_size("wide") * lax.axis_size("narrow")
+    up_blocks = up_grad.astype(jnp.bfloat16).reshape(blocks, -1, up_grad.shape[1])
+    down_blocks = down_grad.astype(jnp.bfloat16).reshape(blocks, -1, channels)
+    up_sum = halving_sum(up_blocks, 0)
+    down_sum = halving_sum(down_blocks, 1)
+    qkv_blocks = qkv_grad.astype(jnp.bfloat16).reshape(blocks, -1, 3 * channels)
+    proj_blocks = proj_grad.astype(jnp.bfloat16).reshape(blocks, -1, channels)
+    taps = jnp.concatenate([conv_attn_grad.reshape(blocks, -1), conv_ffn_grad.reshape(blocks, -1)], 1)
+    rows = qkv_blocks.shape[1]
+    taps_len = taps.shape[1]
+    taps_wide = -(-taps_len // (rows * 128)) * 128
+    taps = jnp.pad(taps, ((0, 0), (0, rows * taps_wide - taps_len)))
+    taps = taps.astype(jnp.bfloat16).reshape(blocks, rows, taps_wide)
+    left_sum = halving_sum(qkv_blocks[:, :, : 2 * channels], 0)
+    right = jnp.concatenate([qkv_blocks[:, :, 2 * channels :], proj_blocks, taps], 2)
+    right_sum = halving_sum(right, 1)
+    qkv_sum = jnp.concatenate([left_sum, right_sum[:, :channels]], 1)
+    proj_sum = right_sum[:, channels : 2 * channels]
+    tap_sums = right_sum[:, 2 * channels :].reshape(-1)
+    attn_len = conv_attn_grad.size // blocks
+    conv_attn_sum = tap_sums[:attn_len].reshape(-1, 9)
+    conv_ffn_sum = tap_sums[attn_len:taps_len].reshape(-1, 9)
     return (
         output.reshape(tokens.shape),
         token_grad,

time: 1030 us -> 608 us (0.59)
  waiting for transfers between devices: 514 us -> 91.6 us
  blocking collectives: 92.1 us -> 0 us
  local copies, waits for them, and re-layouts: 94.3 us -> 151 us
  starting transfers between devices: 14.5 us -> 49.7 us
  other arithmetic: 128 us -> 158 us
  matrix products: 164 us -> 145 us
  between operations: 16.6 us -> 3.75 us
    reduce_scatter x5 -> x0, waiting for transfers between devices: 459 us -> none  [the longest x1 168 us: shards(): lax.psum_scatter(mod_grad, ('wide', 'narrow'), scatter_dimension=0, tiled...]
    unnamed x1 -> x0, blocking collectives: 41.9 us -> none
    ppermute x8 -> x36, waiting for transfers between devices: 29.7 us -> 69.2 us  [from_partner(): lax.ppermute(shard, axis, [(i, i ^ 1 << bit) for i in range(lax.axis_size...]
    all_to_all x2 -> x0, blocking collectives: 37.6 us -> none  [the longest x1 18.9 us: to_groups(): lax.all_to_all(pieces, 'narrow', split_axis=1, concat_axis=1, tiled=True)]
    ppermute x8 -> x36, starting transfers between devices: 4.94 us -> 31.4 us  [from_partner(): lax.ppermute(shard, axis, [(i, i ^ 1 << bit) for i in range(lax.axis_size...]
    convert_element_type x0 -> x16, other arithmetic: none -> 13.6 us  [halving_sum(): held = held.astype(jnp.bfloat16)]
    reshape x0 -> x11, local copies, waits for them, and re-layouts: none -> 13.2 us  [the longest x4 3.82 us: shards(): d_modulation = jnp.stack(flat_parts, 1).reshape(item_count, 6 * channels)]
    dynamic_slice x0 -> x5, local copies, waits for them, and re-layouts: none -> 12.9 us  [the longest x3 9.79 us: halving_sum(): keep = lax.dynamic_index_in_dim(held, mine, where, keepdims=False)]
  transfers between devices with their start and end apart: 16 -> 40, of which waited for: 14 -> 22; matrix products, arithmetic and copies ran while one was open for 22% -> 55% of each run, Pallas kernels for 0% -> 0%
where the time goes in v1:
time: 608 us; the launch traced here: 599 us
  other arithmetic  158 us (26%)
  local copies, waits for them, and re-layouts  151 us (25%)
  matrix products  145 us (24%)
  waiting for transfers between devices  91.6 us (15%)
  starting transfers between devices  49.7 us (8%)
    ppermute x36, waiting for transfers between devices, from_partner(): lax.ppermute(shard, axis, [(i, i ^ 1 << bit) for i in range(lax.axis_size...  69.2 us
    dot_general x1, matrix products, shards(): jnp.einsum('ixyd,fd->ixyf', d_branch_two, w_down, preferred_element_type=...  35.1 us
    ppermute x36, starting transfers between devices, from_partner(): lax.ppermute(shard, axis, [(i, i ^ 1 << bit) for i in range(lax.axis_size...  31.4 us
    concatenate x4, other arithmetic, extend(): return jnp.concatenate([top_rim, widened, bottom_rim], 1)  27.2 us
    unnamed x288, local copies, waits for them, and re-layouts  22.7 us
    another operation x22, local copies, waits for them, and re-layouts, tap_grads(): return jnp.stack(columns, 1)  19.4 us
    convert_element_type x1, other arithmetic, shards(): apply_taps(d_padded_ffn, conv_ffn, half_side, True).astype(jnp.bfloat16)  15.8 us
    add x1, other arithmetic, apply_taps(): summed = summed + window * weights_f[:, stencil]  15.6 us
  transfers between devices with their start and end apart: 40, of which 22 were waited for; matrix products, arithmetic and copies ran while one was open for 55% of the time, Pallas kernels for 0%

profile of v1, /device:TPU:0, one launch (start us, length us, event | category | flops | bytes accessed | tf_op | source)
XLA Modules:
  0.0 598.8 jit_solution(1541009015088107314)
XLA Ops:
  5.1 4.7 fusion.146
  47.6 4.6 all-to-all-start
  55.2 12.9 %all-to-all-done = bf16[3,4,64,768]{3,2,0,1:T(8,128)(2,1)} async-done(((bf16[3,4,64,768]{3,2,0,1:T(8,128)(2,1)}), bf16[3,4,64,768]{3,2,0,1:T(8,128)(2,1)}, u32[]{:S(2)}, u32[]{:S(2)}) %all-to-all-start) | async-done | bytes 1179680 | tf_op jit(solution)/shard_map/all_to_all | solution.py:99
  74.8 5.8 copy.105
  87.9 4.6 fusion.94
  92.5 4.6 reshape_reshape.12
  97.1 5.1 copy.110
  102.2 4.8 all-to-all-start.1
  114.7 8.1 %all-to-all-done.1 = bf16[3,4,64,768]{3,2,0,1:T(8,128)(2,1)} async-done(((bf16[3,4,64,768]{3,2,0,1:T(8,128)(2,1)}), bf16[3,4,64,768]{3,2,0,1:T(8,128)(2,1)}, u32[]{:S(2)}, u32[]{:S(2)}) %all-to-all-start.1) | async-done | bytes 1179680 | tf_op jit(solution)/shard_map/all_to_all | solution.py:106
  130.1 5.0 fusion.142
  149.9 10.7 %collective-permute-done.3 = bf16[3,1,18,3072]{3,2,1,0:T(8,128)(2,1)} collective-permute-done((bf16[3,1,18,3072]{3,2,1,0:T(8,128)(2,1)}, bf16[3,1,18,3072]{3,2,1,0:T(8,128)(2,1)}, u32[]{:S(2)}, u32[]{:S(2)}) %collective-permute-start.3) | collective-permute-done | bytes 331808 | tf_op jit(solution)/shard_map/ppermute | solution.py:16
  161.8 12.1 %maximum_maximum_fusion = (bf16[3,17,18,3072]{3,2,1,0:T(8,128)(2,1)S(1)}, bf16[3,17,18,3072]{3,2,1,0:T(8,128)(2,1)S(1)}) fusion(bf16[3,16,1,3072]{3,2,1,0:T(2,128)(2,1)} %copy-done.27, bf16[3,16,16,3072]{3,2,1,0:T(8,128)(2,1)} %copy-done.5, bf16[3,16,1,3072]{3,2,1,0:T(2,128)(2,1)} %copy-done.25, bf16[3,1,18,3072]{3,2,1,0:T(8,128)(2,1)S(1)} %get-tuple-element.121, ...), kind=kLoop, calls=%fused_computation.61 | loop fusion | flops 45121536 | bytes 17252352 | tf_op jit(solution)/shard_map/concatenate | solution.py:62
  174.1 15.6 %fusion.7 = f32[3,16,16,3072]{3,2,1,0:T(8,128)} fusion(bf16[3,16,16,3072]{3,2,1,0:T(8,128)(2,1)S(1)} %bitcast.307, bf16[3,16,1,3072]{3,2,1,0:T(2,128)(2,1)} %copy-done.27, bf16[3,16,1,3072]{3,2,1,0:T(2,128)(2,1)S(1)} %copy-done.26, f32[3072]{0:T(1024)S(1)} %bitcast.354, f32[3072]{0:T(1024)S(1)} %bitcast.352, f32[3072]{0:T(1024)S(1)} %bitcast.350, ...), kind=kLoop, calls=%fused_computation.28 | loop fusion | flops 75497472 | bytes 43167744 | tf_op jit(solution)/shard_map/add | solution.py:77
  189.7 35.1 %fusion.29 = (bf16[3072]{0:T(1024)(128)(2,1)}, bf16[3072]{0:T(1024)(128)(2,1)}, bf16[3072]{0:T(1024)(128)(2,1)}, bf16[3072]{0:T(1024)(128)(2,1)}, bf16[3072]{0:T...) fusion(bf16[3,17,18,3072]{3,2,1,0:T(8,128)(2,1)} %copy-done.4, ...), kind=kOutput, calls=%fused_computation.50 | convolution fusion | flops 3753612288 | bytes 53738508 | tf_op jit(solution)/shard_map/ixyd,fd->ixyf/dot_general | solution.py:228
  237.7 9.7 %bitcast_convert_fusion = bf16[3072,768]{1,0:T(8,128)(2,1)} fusion(bf16[3,16,16,768]{3,2,1,0:T(8,128)(2,1)S(1)} %bitcast.359, f32[3]{0:T(128)S(1)} %compare_convert_fusion, f32[3,768]{1,0:T(4,128)S(1)} %copy-done.112, f32[3,16,16,3072]{3,2,1,0:T(8,128)} %fusion.7), kind=kOutput, calls=%fused_computation.51 | convolution fusion | flops 3649830912 | bytes 15344652 | tf_op jit(solution)/shard_map/ixyf,ixyd->fd/dot_general | solution.py:225
  267.8 10.0 %pad_maximum_fusion.1 = (bf16[3,17,18,3072]{3,2,1,0:T(8,128)(2,1)S(1)}, bf16[3,17,18,3072]{3,2,1,0:T(8,128)(2,1)S(1)}) fusion(bf16[3,1,18,3072]{3,2,1,0:T(8,128)(2,1)S(1)} %get-tuple-element.119, bf16[3,16,1,3072]{3,2,1,0:T(2,128)(2,1)S(1)} %copy-done.31, bf16[3,16,16,3072]{3,2,1,0:T(8,128)(2,1)S(1)} %bitcast.305, ...), kind=kLoop, calls=%fused_computation.63 | loop fusion | flops 45121536 | bytes 17252352 | tf_op jit(solution)/shard_map/concatenate | solution.py:62
  278.0 15.8 %fusion.20 = bf16[3,16,16,3072]{3,2,1,0:T(8,128)(2,1)} fusion(bf16[3,16,16,3072]{3,2,1,0:T(8,128)(2,1)S(1)} %bitcast.305, bf16[3,17,18,3072]{3,2,1,0:T(8,128)(2,1)S(1)} %get-tuple-element.100, bf16[3,16,1,3072]{3,2,1,0:T(2,128)(2,1)S(1)} %copy-done.29, bf16[3,16,1,3072]{3,2,1,0:T(2,128)(2,1)} %copy-done.30, ...), kind=kLoop, calls=%fused_computation.41 | loop fusion | flops 77856768 | bytes 38449152 | tf_op jit(solution)/shard_map/convert_element_type | solution.py:238
  293.9 8.6 %multiply_reduce_fusion.5 = (f32[3,16,16]{2,1,0:T(8,128)S(1)}, f32[3,16,16,768]{3,2,1,0:T(8,128)S(1)}) fusion(f32[3,16,16,768]{3,2,1,0:T(8,128)} %copy-done.12, f32[3,768]{1,0:T(4,128)S(1)} %copy-done.93, f32[3,16,16]{2,1,0:T(8,128)S(1)} %copy-done.53, bf16[3,16,16,3072]{3,2,1,0:T(8,128)(2,1)} %fusion.20, bf16[768,3072]{1,0:T(8,128)(2,1)} %param.17), kind=kOutput, calls=%fused_computation.170 | convolution fusion | flops 3626237184 | bytes 14171136 | tf_op jit(solution)/shard_map/ixyf,df->ixyd/dot_general | solution.py:240
  302.6 6.4 %bitcast_convert_fusion.1 = bf16[768,3072]{1,0:T(8,128)(2,1)} fusion(bf16[3,16,16,3072]{3,2,1,0:T(8,128)(2,1)S(1)} %copy-done.33, f32[3,16,16,768]{3,2,1,0:T(8,128)S(1)} %copy-done.13, f32[3,768]{1,0:T(4,128)S(1)} %copy-done.115, f32[3,768]{1,0:T(4,128)S(1)} %copy-done.93, f32[3,16,16]{2,1,0:T(8,128)S(1)} %copy-done.81, f32[3,16,16]{2,1,0:T(8,128)S(1)} %copy-done.53), kind=kOutput, calls=%fused_computation.52 | convolution fusion | flops 3629187072 | bytes 11821056 | tf_op jit(solution)/shard_map/ixyd,ixyf->df/dot_general | solution.py:239
  311.5 10.4 %fusion.86 = (f32[3,768]{1,0:T(4,128)}, bf16[3,16,16,768]{3,2,1,0:T(8,128)(2,1)}, f32[3,768]{1,0:T(4,128)}, f32[3,16,16,768]{3,2,1,0:T(8,128)S(1)}) fusion(bf16[3,16,16,768]{3,2,1,0:T(8,128)(2,1)S(1)} %bitcast.360, f32[3]{0:T(128)S(1)} %compare_convert_fusion, f32[3,16,16,768]{3,2,1,0:T(8,128)S(1)} %copy-done.13, f32[3,768]{1,0:T(4,128)S(1)} %copy-done.113, ...), kind=kOutput, calls=%fused_computation.159 | convolution fusion | flops 3655724544 | bytes 26001420 | tf_op jit(solution)/shard_map/dot_general | solution.py:218
  352.0 5.2 copy.121
  361.7 6.8 %fusion.87 = bf16[3,256,1,12,64]{1,4,3,0,2:T(8,128)(2,1)} fusion(bf16[3,256,12,64]{1,3,2,0:T(8,128)(2,1)} %reshape_reshape.13, f32[3,12,256,256]{2,3,1,0:T(8,128)} %copy-done.1, f32[3,12,256]{2,1,0:T(8,128)} %log_add_fusion), kind=kOutput, calls=%fused_computation.182 | convolution fusion | flops 309067776 | bytes 11833344 | tf_op jit(solution)/shard_map/ihqk,iqhe->ikhe/dot_general | solution.py:255
  368.5 8.2 %multiply_reduce_fusion = (f32[3,12,256]{2,1,0:T(8,128)}, f32[3,12,256,256]{2,3,1,0:T(8,128)}) fusion(f32[3,12,256,256]{2,3,1,0:T(8,128)} %copy-done.1, f32[3,12,256]{2,1,0:T(8,128)S(1)} %copy-done.46, bf16[3,256,12,64]{1,3,2,0:T(8,128)(2,1)S(1)} %copy-done.15, bf16[3,256,3,12,64]{1,4,3,2,0:T(8,128)(2,1)} %bitcast.310), kind=kOutput, calls=%fused_computation.54 | convolution fusion | flops 311417856 | bytes 21307392 | tf_op jit(solution)/shard_map/iqhe,ikhe->ihqk/dot_general | solution.py:254
  376.8 11.3 %multiply_convert_fusion = bf16[3,12,256,256]{2,3,1,0:T(8,128)(2,1)} fusion(f32[3,12,256,256]{2,3,1,0:T(8,128)} %get-tuple-element.170, f32[3,12,256,256]{2,3,1,0:T(8,128)} %copy-done.1, f32[3,12,256]{2,1,0:T(8,128)} %get-tuple-element.169, f32[3,12,256]{2,1,0:T(8,128)} %log_add_fusion), kind=kLoop, calls=%fused_computation.53 | loop fusion | flops 11796480 | bytes 23666688 | tf_op jit(solution)/shard_map/convert_element_type | solution.py:258
  404.3 5.3 bitcast_convert_fusion.2
  430.0 7.7 %fusion.78 = (bf16[768]{0:T(1024)(128)(2,1)}, bf16[768]{0:T(1024)(128)(2,1)}, bf16[768]{0:T(1024)(128)(2,1)}, bf16[768]{0:T(1024)(128)(2,1)S(1)}, bf16[768]{0:T(...) fusion(bf16[3,16,16,768]{3,2,1,0:T(8,128)(2,1)} %reshape.319, ...), kind=kLoop, calls=%fused_computation.144 | loop fusion | flops 18278400 | bytes 9596928 | tf_op jit(solution)/shard_map/reduce_sum | solution.py:90
  489.4 4.9 fusion.125
  494.3 5.7 fusion.134
  513.2 9.0 %collective-permute-done.15 = f32[4,3,4608]{2,1,0:T(4,128)S(1)} collective-permute-done((f32[4,3,4608]{2,1,0:T(4,128)S(1)}, f32[4,3,4608]{2,1,0:T(4,128)S(1)}, u32[]{:S(2)}, u32[]{:S(2)}) %collective-permute-start.15) | collective-permute-done | bytes 221216 | tf_op jit(solution)/shard_map/ppermute | solution.py:16
  549.5 7.4 %collective-permute-done.33 = bf16[2,2,96,768]{3,2,0,1:T(8,128)(2,1)S(1)} collective-permute-done((bf16[2,2,96,768]{3,2,0,1:T(8,128)(2,1)S(1)}, bf16[2,2,96,768]{3,2,0,1:T(8,128)(2,1)S(1)}, u32[]{:S(2)}, u32[]{:S(2)}) %collective-permute-start.33) | collective-permute-done | bytes 589856 | tf_op jit(solution)/shard_map/ppermute | solution.py:16
  566.9 5.4 collective-permute-done.35
  573.2 4.6 collective-permute-done.28
  (540 shorter events, 318.7 us)
Async XLA Ops:
  26.5 6.3 %collective-permute-start.1 = (bf16[3,1,18,768]{3,2,1,0:T(8,128)(2,1)S(1)}, bf16[3,1,18,768]{3,2,1,0:T(8,128)(2,1)S(1)}, u32[]{:S(2)}, u32[]{:S(2)}) collective-permute-start(bf16[3,1,18,768]{3,2,1,0:T(8,128)(2,1)S(1)} %fusion.121), channel_id=1, source_target_pairs={{0,2},{1,3},{2,0},{3,1},{4,6},{5,7},{6,4},{7,5},{8,10},{9,11},{10,... | collective-permute-start | bytes 248840 | tf_op jit(solution)/shard_map/ppermute | solution.py:16
  47.6 20.4 %all-to-all-start = ((bf16[3,4,64,768]{3,2,0,1:T(8,128)(2,1)}), bf16[3,4,64,768]{3,2,0,1:T(8,128)(2,1)}, u32[]{:S(2)}, u32[]{:S(2)}) async-start(bf16[3,4,64,768]{3,2,0,1:T(8,128)(2,1)} %bitcast.322), calls=%async_computation | async-start | bytes 2359296 | tf_op jit(solution)/shard_map/all_to_all | solution.py:99
  53.5 57.5 %collective-permute-start.10 = (bf16[1,3,768]{2,1,0:T(4,128)(2,1)}, bf16[1,3,768]{2,1,0:T(4,128)(2,1)}, u32[]{:S(2)}, u32[]{:S(2)}) collective-permute-start(bf16[1,3,768]{2,1,0:T(4,128)(2,1)} %fusion.163), channel_id=1, source_target_pairs={{0,4},{4,0},{8,12},{12,8},{16,20},{20,16},{24,28},{28,24},{1,5},{5... | collective-permute-start | bytes 13832 | tf_op jit(solution)/shard_map/ppermute | solution.py:16
  102.2 20.7 %all-to-all-start.1 = ((bf16[3,4,64,768]{3,2,0,1:T(8,128)(2,1)}), bf16[3,4,64,768]{3,2,0,1:T(8,128)(2,1)}, u32[]{:S(2)}, u32[]{:S(2)}) async-start(bf16[3,4,64,768]{3,2,0,1:T(8,128)(2,1)} %copy.110), calls=%async_computation.1 | async-start | bytes 2359296 | tf_op jit(solution)/shard_map/all_to_all | solution.py:106
  112.9 28.7 %collective-permute-start.11 = (bf16[2,3,768]{2,1,0:T(4,128)(2,1)}, bf16[2,3,768]{2,1,0:T(4,128)(2,1)}, u32[]{:S(2)}, u32[]{:S(2)}) collective-permute-start(bf16[2,3,768]{2,1,0:T(4,128)(2,1)} %pad_maximum_fusion.27), channel_id=1, source_target_pairs={{0,8},{4,12},{8,0},{12,4},{16,24},{20,28},{24,16},{28,20},{1,9},{5... | collective-permute-start | bytes 27656 | tf_op jit(solution)/shard_map/ppermute | solution.py:16
  148.0 12.6 %collective-permute-start.3 = (bf16[3,1,18,3072]{3,2,1,0:T(8,128)(2,1)}, bf16[3,1,18,3072]{3,2,1,0:T(8,128)(2,1)}, u32[]{:S(2)}, u32[]{:S(2)}) collective-permute-start(bf16[3,1,18,3072]{3,2,1,0:T(8,128)(2,1)} %fusion.110), channel_id=1, source_target_pairs={{0,2},{1,3},{2,0},{3,1},{4,6},{5,7},{6,4},{7,5},{8,10},{9,11},{10,... | collective-permute-start | bytes 995336 | tf_op jit(solution)/shard_map/ppermute | solution.py:16
  237.2 29.4 %collective-permute-start.5 = (bf16[3,1,18,3072]{3,2,1,0:T(8,128)(2,1)}, bf16[3,1,18,3072]{3,2,1,0:T(8,128)(2,1)}, u32[]{:S(2)}, u32[]{:S(2)}) collective-permute-start(bf16[3,1,18,3072]{3,2,1,0:T(8,128)(2,1)} %fusion.109), channel_id=1, source_target_pairs={{0,2},{1,3},{2,0},{3,1},{4,6},{5,7},{6,4},{7,5},{8,10},{9,11},{10,... | collective-permute-start | bytes 995336 | tf_op jit(solution)/shard_map/ppermute | solution.py:16
  266.4 146.1 %collective-permute-start.31 = (bf16[2,2,2,2,96,768]{5,4,0,1,2,3:T(8,128)(2,1)}, bf16[2,2,2,2,96,768]{5,4,0,1,2,3:T(8,128)(2,1)}, u32[]{:S(2)}, u32[]{:S(2)}) collective-permute-start(bf16[2,2,2,2,96,768]{5,4,0,1,2,3:T(8,128)(2,1)} %bitcast.295), channel_id=1, source_target_pairs={{0,1},{1,0},{2,3},{3,2},{4,5},{5,4},{6,7},{7,6},{8,9},{9,8},{10,11... | collective-permute-start | bytes 7077896 | tf_op jit(solution)/shard_map/ppermute | solution.py:16
  331.7 20.4 %all-to-all-start.2 = ((bf16[3,4,64,768]{3,2,0,1:T(8,128)(2,1)}), bf16[3,4,64,768]{3,2,0,1:T(8,128)(2,1)}, u32[]{:S(2)}, u32[]{:S(2)}) async-start(bf16[3,4,64,768]{3,2,0,1:T(8,128)(2,1)} %bitcast.321), calls=%async_computation.2 | async-start | bytes 2359296 | tf_op jit(solution)/shard_map/all_to_all | solution.py:99
  347.1 160.6 %collective-permute-start.26 = (bf16[2,2,2,2,24,3072]{5,4,0,1,3,2:T(8,128)(2,1)}, bf16[2,2,2,2,24,3072]{5,4,0,1,3,2:T(8,128)(2,1)}, u32[]{:S(2)}, u32[]{:S(2)}) collective-permute-start(bf16[2,2,2,2,24,3072]{5,4,0,1,3,2:T(8,128)(2,1)} %bitcast.296), channel_id=1, source_target_pairs={{0,1},{1,0},{2,3},{3,2},{4,5},{5,4},{6,7},{7,6},{8,9},{9,8},{10,11... | collective-permute-start | bytes 7077896 | tf_op jit(solution)/shard_map/ppermute | solution.py:16
  399.8 20.9 %all-to-all-start.3 = ((bf16[3,4,64,768]{3,2,0,1:T(8,128)(2,1)}), bf16[3,4,64,768]{3,2,0,1:T(8,128)(2,1)}, u32[]{:S(2)}, u32[]{:S(2)}) async-start(bf16[3,4,64,768]{3,2,0,1:T(8,128)(2,1)} %copy.127), calls=%async_computation.3 | async-start | bytes 2359296 | tf_op jit(solution)/shard_map/all_to_all | solution.py:106
  412.0 88.0 %collective-permute-start.16 = (bf16[2,2,2,2,24,1536]{5,4,3,2,1,0:T(8,128)(2,1)}, bf16[2,2,2,2,24,1536]{5,4,3,2,1,0:T(8,128)(2,1)}, u32[]{:S(2)}, u32[]{:S(2)}) collective-permute-start(bf16[2,2,2,2,24,1536]{5,4,3,2,1,0:T(8,128)(2,1)} %dynamic-slice_bitcast_fusion.2), channel_id=1, source_target_pairs={{0,1},{1,0},{2,3},{3,2},{4,5},{5,4},{6,7},{7,6},{8,9},{9,8},{10,11... | collective-permute-start | bytes 3538952 | tf_op jit(solution)/shard_map/ppermute | solution.py:16
  418.7 113.7 %collective-permute-start.32 = (bf16[2,2,2,96,768]{4,3,0,1,2:T(8,128)(2,1)}, bf16[2,2,2,96,768]{4,3,0,1,2:T(8,128)(2,1)}, u32[]{:S(2)}, u32[]{:S(2)}) collective-permute-start(bf16[2,2,2,96,768]{4,3,0,1,2:T(8,128)(2,1)} %dynamic-slice_bitcast_fusion), channel_id=1, source_target_pairs={{0,2},{1,3},{2,0},{3,1},{4,6},{5,7},{6,4},{7,5},{8,10},{9,11},{10,... | collective-permute-start | bytes 3538952 | tf_op jit(solution)/shard_map/ppermute | solution.py:16
  437.7 24.8 %collective-permute-start.6 = (bf16[3,16,1,768]{3,2,1,0:T(2,128)(2,1)}, bf16[3,16,1,768]{3,2,1,0:T(2,128)(2,1)}, u32[]{:S(2)}, u32[]{:S(2)}) collective-permute-start(bf16[3,16,1,768]{3,2,1,0:T(2,128)(2,1)} %broadcast_select_fusion.11), channel_id=1, source_target_pairs={{0,1},{1,0},{2,3},{3,2},{4,5},{5,4},{6,7},{7,6},{8,9},{9,8},{10,11... | collective-permute-start | bytes 221192 | tf_op jit(solution)/shard_map/ppermute | solution.py:16
  463.8 5.5 collective-permute-start.7
  466.5 72.2 %collective-permute-start.21 = (bf16[2,2,2,2,24,1664]{5,4,0,1,2,3:T(8,128)(2,1)}, bf16[2,2,2,2,24,1664]{5,4,0,1,2,3:T(8,128)(2,1)}, u32[]{:S(2)}, u32[]{:S(2)}) collective-permute-start(bf16[2,2,2,2,24,1664]{5,4,0,1,2,3:T(8,128)(2,1)} %bitcast.297), channel_id=1, source_target_pairs={{0,1},{1,0},{2,3},{3,2},{4,5},{5,4},{6,7},{7,6},{8,9},{9,8},{10,11... | collective-permute-start | bytes 3833864 | tf_op jit(solution)/shard_map/ppermute | solution.py:16
  487.8 13.8 %collective-permute-start.13 = (f32[1,3,4608]{2,1,0:T(4,128)S(1)}, f32[1,3,4608]{2,1,0:T(4,128)S(1)}, u32[]{:S(2)}, u32[]{:S(2)}) collective-permute-start(f32[1,3,4608]{2,1,0:T(4,128)S(1)} %bitcast.328), channel_id=1, source_target_pairs={{0,4},{4,0},{8,12},{12,8},{16,20},{20,16},{24,28},{28,24},{1,5},{5... | collective-permute-start | bytes 165896 | tf_op jit(solution)/shard_map/ppermute | solution.py:16
  501.7 5.4 collective-permute-start.14
  504.2 24.9 %collective-permute-start.17 = (bf16[2,2,2,24,1536]{4,3,2,1,0:T(8,128)(2,1)}, bf16[2,2,2,24,1536]{4,3,2,1,0:T(8,128)(2,1)}, u32[]{:S(2)}, u32[]{:S(2)}) collective-permute-start(bf16[2,2,2,24,1536]{4,3,2,1,0:T(8,128)(2,1)} %dynamic-slice_bitcast_fusion.6), channel_id=1, source_target_pairs={{0,4},{4,0},{8,12},{12,8},{16,20},{20,16},{24,28},{28,24},{1,5},{5... | collective-permute-start | bytes 1769480 | tf_op jit(solution)/shard_map/ppermute | solution.py:16
  507.3 15.0 %collective-permute-start.15 = (f32[4,3,4608]{2,1,0:T(4,128)S(1)}, f32[4,3,4608]{2,1,0:T(4,128)S(1)}, u32[]{:S(2)}, u32[]{:S(2)}) collective-permute-start(f32[4,3,4608]{2,1,0:T(4,128)S(1)} %pad_maximum_fusion.18), channel_id=1, source_target_pairs={{0,16},{4,20},{8,24},{12,28},{16,0},{20,4},{24,8},{28,12},{1,17},{... | collective-permute-start | bytes 663560 | tf_op jit(solution)/shard_map/ppermute | solution.py:16
  512.8 44.9 %collective-permute-start.27 = (bf16[2,2,2,24,3072]{4,3,0,1,2:T(8,128)(2,1)}, bf16[2,2,2,24,3072]{4,3,0,1,2:T(8,128)(2,1)}, u32[]{:S(2)}, u32[]{:S(2)}) collective-permute-start(bf16[2,2,2,24,3072]{4,3,0,1,2:T(8,128)(2,1)} %dynamic-slice_bitcast_fusion.1), channel_id=1, source_target_pairs={{0,4},{4,0},{8,12},{12,8},{16,20},{20,16},{24,28},{28,24},{1,5},{5... | collective-permute-start | bytes 3538952 | tf_op jit(solution)/shard_map/ppermute | solution.py:16
  530.6 8.0 %collective-permute-start.18 = (bf16[2,2,24,1536]{3,2,1,0:T(8,128)(2,1)S(1)}, bf16[2,2,24,1536]{3,2,1,0:T(8,128)(2,1)S(1)}, u32[]{:S(2)}, u32[]{:S(2)}) collective-permute-start(bf16[2,2,24,1536]{3,2,1,0:T(8,128)(2,1)S(1)} %dynamic-slice_bitcast_fusion.10), channel_id=1, source_target_pairs={{0,2},{1,3},{2,0},{3,1},{4,6},{5,7},{6,4},{7,5},{8,10},{9,11},{10,... | collective-permute-start | bytes 884744 | tf_op jit(solution)/shard_map/ppermute | solution.py:16
  534.0 23.0 %collective-permute-start.33 = (bf16[2,2,96,768]{3,2,0,1:T(8,128)(2,1)S(1)}, bf16[2,2,96,768]{3,2,0,1:T(8,128)(2,1)S(1)}, u32[]{:S(2)}, u32[]{:S(2)}) collective-permute-start(bf16[2,2,96,768]{3,2,0,1:T(8,128)(2,1)S(1)} %dynamic-slice_bitcast_fusion.4), channel_id=1, source_target_pairs={{0,4},{4,0},{8,12},{12,8},{16,20},{20,16},{24,28},{28,24},{1,5},{5... | collective-permute-start | bytes 1769480 | tf_op jit(solution)/shard_map/ppermute | solution.py:16
  543.9 5.6 collective-permute-start.20
  545.0 14.9 %collective-permute-start.22 = (bf16[2,2,2,24,1664]{4,3,0,1,2:T(8,128)(2,1)S(1)}, bf16[2,2,2,24,1664]{4,3,0,1,2:T(8,128)(2,1)S(1)}, u32[]{:S(2)}, u32[]{:S(2)}) collective-permute-start(bf16[2,2,2,24,1664]{4,3,0,1,2:T(8,128)(2,1)S(1)} %dynamic-slice_bitcast_fusion.3), channel_id=1, source_target_pairs={{0,2},{1,3},{2,0},{3,1},{4,6},{5,7},{6,4},{7,5},{8,10},{9,11},{10,... | collective-permute-start | bytes 1916936 | tf_op jit(solution)/shard_map/ppermute | solution.py:16
  557.1 7.5 %collective-permute-start.34 = (bf16[2,96,768]{2,1,0:T(8,128)(2,1)S(1)}, bf16[2,96,768]{2,1,0:T(8,128)(2,1)S(1)}, u32[]{:S(2)}, u32[]{:S(2)}) collective-permute-start(bf16[2,96,768]{2,1,0:T(8,128)(2,1)S(1)} %dynamic-slice_bitcast_fusion.8), channel_id=1, source_target_pairs={{0,8},{4,12},{8,0},{12,4},{16,24},{20,28},{24,16},{28,20},{1,9},{5... | collective-permute-start | bytes 884744 | tf_op jit(solution)/shard_map/ppermute | solution.py:16
  560.1 12.9 %collective-permute-start.23 = (bf16[2,2,24,1664]{3,2,0,1:T(8,128)(2,1)S(1)}, bf16[2,2,24,1664]{3,2,0,1:T(8,128)(2,1)S(1)}, u32[]{:S(2)}, u32[]{:S(2)}) collective-permute-start(bf16[2,2,24,1664]{3,2,0,1:T(8,128)(2,1)S(1)} %dynamic-slice_bitcast_fusion.7), channel_id=1, source_target_pairs={{0,4},{4,0},{8,12},{12,8},{16,20},{20,16},{24,28},{28,24},{1,5},{5... | collective-permute-start | bytes 958472 | tf_op jit(solution)/shard_map/ppermute | solution.py:16
  564.7 7.6 %collective-permute-start.35 = (bf16[96,768]{1,0:T(8,128)(2,1)S(1)}, bf16[96,768]{1,0:T(8,128)(2,1)S(1)}, u32[]{:S(2)}, u32[]{:S(2)}) collective-permute-start(bf16[96,768]{1,0:T(8,128)(2,1)S(1)} %dynamic-slice_bitcast_fusion.12), channel_id=1, source_target_pairs={{0,16},{4,20},{8,24},{12,28},{16,0},{20,4},{24,8},{28,12},{1,17},{... | collective-permute-start | bytes 442376 | tf_op jit(solution)/shard_map/ppermute | solution.py:16
  565.2 12.6 %collective-permute-start.28 = (bf16[2,2,24,3072]{3,2,0,1:T(8,128)(2,1)S(1)}, bf16[2,2,24,3072]{3,2,0,1:T(8,128)(2,1)S(1)}, u32[]{:S(2)}, u32[]{:S(2)}) collective-permute-start(bf16[2,2,24,3072]{3,2,0,1:T(8,128)(2,1)S(1)} %dynamic-slice_bitcast_fusion.5), channel_id=1, source_target_pairs={{0,2},{1,3},{2,0},{3,1},{4,6},{5,7},{6,4},{7,5},{8,10},{9,11},{10,... | collective-permute-start | bytes 1769480 | tf_op jit(solution)/shard_map/ppermute | solution.py:16
  578.6 5.7 collective-permute-start.25
  580.7 6.8 %collective-permute-start.29 = (bf16[2,24,3072]{2,1,0:T(8,128)(2,1)S(1)}, bf16[2,24,3072]{2,1,0:T(8,128)(2,1)S(1)}, u32[]{:S(2)}, u32[]{:S(2)}) collective-permute-start(bf16[2,24,3072]{2,1,0:T(8,128)(2,1)S(1)} %dynamic-slice_bitcast_fusion.9), channel_id=1, source_target_pairs={{0,8},{4,12},{8,0},{12,4},{16,24},{20,28},{24,16},{28,20},{1,9},{5... | collective-permute-start | bytes 884744 | tf_op jit(solution)/shard_map/ppermute | solution.py:16
  589.0 7.9 %collective-permute-start.30 = (bf16[24,3072]{1,0:T(8,128)(2,1)}, bf16[24,3072]{1,0:T(8,128)(2,1)}, u32[]{:S(2)}, u32[]{:S(2)}) collective-permute-start(bf16[24,3072]{1,0:T(8,128)(2,1)} %dynamic-slice_bitcast_fusion.13), channel_id=1, source_target_pairs={{0,16},{4,20},{8,24},{12,28},{16,0},{20,4},{24,8},{28,12},{1,17},{... | collective-permute-start | bytes 442376 | tf_op jit(solution)/shard_map/ppermute | solution.py:16
  (148 other events, 1106.3 us)

commit v2 on v1

--- a/solution.py
+++ b/solution.py
@@ -1,8 +1,11 @@
+import functools
 import math
 
 import jax
 import jax.numpy as jnp
 from jax import lax
+from jax.experimental import pallas as pl
+from jax.experimental.pallas import tpu as pltpu
 from jax.sharding import PartitionSpec as P
 
 HEADS = 12
@@ -27,23 +30,11 @@
     return normed(field_map) * (1.0 + scale) + shift
 
 
-def gelu_tanh(field_map):
-    return jax.nn.gelu(field_map, approximate=True)
-
-
 def attn_across(outgoing):
     return from_partner(outgoing, "narrow", 0)
 
 
 def attn_down(outgoing):
-    return from_partner(outgoing, "narrow", 1)
-
-
-def ffn_across(outgoing):
-    return from_partner(outgoing, "narrow", 0)
-
-
-def ffn_down(outgoing):
     return from_partner(outgoing, "narrow", 1)
 
 
@@ -172,6 +163,282 @@
     return held
 
 
+LANES = 128
+INSET = 8
+GELU_SCALE = math.sqrt(2.0 / math.pi)
+GELU_CUBE = 0.044715
+
+
+def rim_exchange(field_map, row_half, col_half):
+    column = jnp.where(col_half == 0, field_map[:, :, -1], field_map[:, :, 0])
+    row = jnp.where(row_half == 0, field_map[:, -1], field_map[:, 0])
+    point = jnp.where(col_half == 0, row[:, -1:], row[:, :1])
+    size = lax.axis_size("narrow")
+    column = lax.ppermute(column, "narrow", [(i, i ^ 1) for i in range(size)])
+    row = lax.ppermute(row, "narrow", [(i, i ^ 2) for i in range(size)])
+    point = lax.ppermute(point, "narrow", [(i, i ^ 3) for i in range(size)])
+    upper = row_half == 1
+    left = col_half == 1
+
+    def kept(values, where):
+        return jnp.where(where, values, jnp.zeros_like(values))
+
+    spare = jnp.zeros((point.shape[0], 4) + point.shape[2:], point.dtype)
+    return jnp.concatenate(
+        [
+            kept(column, left),
+            kept(column, ~left),
+            kept(row, upper),
+            kept(row, ~upper),
+            kept(point, upper & left),
+            kept(point, upper & ~left),
+            kept(point, ~upper & left),
+            kept(point, ~upper & ~left),
+            spare,
+        ],
+        1,
+    )
+
+
+def fill_padded(padded, inner, rim, items, side):
+    high = side + 2
+    area = side * side
+    count = 4 * side + 8
+    for item in range(items):
+        top = item * high
+        block = inner[item * area : (item + 1) * area]
+        padded[top + 1 : top + 1 + side, INSET : INSET + side, :] = block.reshape(side, side, -1)
+        base = item * count
+        padded[top, INSET : INSET + side, :] = rim[base + 2 * side : base + 3 * side, :]
+        padded[top + side + 1, INSET : INSET + side, :] = rim[base + 3 * side : base + 4 * side, :]
+        for corner, (row, col) in enumerate(
+            [(0, INSET - 1), (0, INSET + side), (side + 1, INSET - 1), (side + 1, INSET + side)]
+        ):
+            at = base + 4 * side + corner
+            padded[top + row, col : col + 1, :] = rim[at : at + 1, :]
+        for row in range(side):
+            padded[top + 1 + row, INSET - 1 : INSET, :] = rim[base + row : base + row + 1, :]
+            at = base + side + row
+            padded[top + 1 + row, INSET + side : INSET + side + 1, :] = rim[at : at + 1, :]
+
+
+def ffn_kernel(
+    items,
+    side,
+    second_ref,
+    rim_ref,
+    d_two_ref,
+    w_up_ref,
+    w_down_ref,
+    taps_ref,
+    two_ref,
+    d_filtered_ref,
+    down_ref,
+    tap_grad_ref,
+    padded,
+    rim,
+    act,
+    d_act,
+):
+    chunk = w_up_ref.shape[1]
+    low = jnp.bfloat16
+    raised = jnp.dot(second_ref[...], w_up_ref[...], preferred_element_type=jnp.float32)
+    rim[...] = (
+        jnp.dot(rim_ref[...], w_up_ref[...], preferred_element_type=jnp.float32)
+        .astype(low)
+        .astype(jnp.float32)
+    )
+    fill_padded(padded, raised.astype(low).astype(jnp.float32), rim, items, side)
+    d_act[...] = lax.dot_general(
+        d_two_ref[...], w_down_ref[...], (((1,), (1,)), ((), ())), preferred_element_type=jnp.float32
+    )
+    for lane in range(0, chunk, LANES):
+        lanes = slice(lane, lane + LANES)
+        weights = [taps_ref[tap : tap + 1, lanes] for tap in range(9)]
+        sums = tuple(jnp.zeros((8, LANES), jnp.float32) for _ in range(9))
+        for item in range(items):
+
+            def one_row(row, sums, item=item):
+                top = item * (side + 2) + row
+                at = pl.ds(pl.multiple_of(item * side * side + row * side, side), side)
+                windows = [
+                    padded[top + tap // 3, INSET - 1 + tap % 3 : INSET - 1 + tap % 3 + side, lanes]
+                    for tap in range(9)
+                ]
+                v = windows[0] * weights[0]
+                for tap in range(1, 9):
+                    v = v + windows[tap] * weights[tap]
+                square = v * v
+                bend = jnp.tanh(GELU_SCALE * v * (1.0 + GELU_CUBE * square))
+                half = 0.5 + 0.5 * bend
+                act[at, lanes] = (v * half).astype(low)
+                slope = half + 0.5 * v * (1.0 - bend * bend) * (
+                    GELU_SCALE + (3.0 * GELU_CUBE * GELU_SCALE) * square
+                )
+                rounded = (d_act[at, lanes] * slope).astype(low)
+                d_filtered_ref[at, lanes] = rounded
+                wide = rounded.astype(jnp.float32)
+                added = []
+                for tap in range(9):
+                    product = windows[tap] * wide
+                    total = sums[tap]
+                    for part in range(0, side, 8):
+                        total = total + product[part : part + 8]
+                    added.append(total)
+                return tuple(added)
+
+            sums = lax.fori_loop(0, side, one_row, sums)
+        for tap in range(9):
+            tap_grad_ref[tap : tap + 1, lanes] = jnp.sum(sums[tap], 0, keepdims=True)
+    tap_grad_ref[9:, :] = jnp.zeros((tap_grad_ref.shape[0] - 9, chunk), jnp.float32)
+    down_ref[...] = lax.dot_general(
+        act[...], d_two_ref[...], (((0,), (0,)), ((), ())), preferred_element_type=jnp.float32
+    ).astype(low)
+    part_two = jnp.dot(act[...], w_down_ref[...], preferred_element_type=jnp.float32)
+
+    @pl.when(pl.program_id(0) == 0)
+    def _():
+        two_ref[...] = part_two
+
+    @pl.when(pl.program_id(0) > 0)
+    def _():
+        two_ref[...] += part_two
+
+
+def ffn_back_kernel(
+    items,
+    side,
+    d_filtered_ref,
+    rim_ref,
+    flipped_ref,
+    w_up_ref,
+    taps_ref,
+    up_ref,
+    d_second_ref,
+    padded,
+    rim,
+    d_raised,
+):
+    chunk = w_up_ref.shape[1]
+    low = jnp.bfloat16
+    rim[...] = rim_ref[...].astype(jnp.float32)
+    fill_padded(padded, d_filtered_ref[...].astype(jnp.float32), rim, items, side)
+    for lane in range(0, chunk, LANES):
+        lanes = slice(lane, lane + LANES)
+        weights = [taps_ref[8 - tap : 9 - tap, lanes] for tap in range(9)]
+        for item in range(items):
+
+            def one_row(row, carry, item=item):
+                top = item * (side + 2) + row
+                at = pl.ds(pl.multiple_of(item * side * side + row * side, side), side)
+                v = None
+                for tap in range(9):
+                    first = INSET - 1 + tap % 3
+                    term = padded[top + tap // 3, first : first + side, lanes] * weights[tap]
+                    v = term if v is None else v + term
+                d_raised[at, lanes] = v.astype(low)
+                return carry
+
+            lax.fori_loop(0, side, one_row, 0)
+    up_ref[...] = jnp.dot(
+        flipped_ref[...], d_raised[...], preferred_element_type=jnp.float32
+    ).astype(low)
+    part = lax.dot_general(
+        d_raised[...], w_up_ref[...], (((1,), (1,)), ((), ())), preferred_element_type=jnp.float32
+    )
+
+    @pl.when(pl.program_id(0) == 0)
+    def _():
+        d_second_ref[...] = part
+
+    @pl.when(pl.program_id(0) > 0)
+    def _():
+        d_second_ref[...] += part
+
+
+def ffn_pass(second, rim, d_two, w_up, w_down, taps, items, side, chunk=256):
+    tokens, channels = second.shape
+    wide = w_up.shape[1]
+    rims = rim.shape[0]
+    fixed = lambda step: (0, 0)
+    columns = lambda step: (0, step)
+    rows = lambda step: (step, 0)
+    return pl.pallas_call(
+        functools.partial(ffn_kernel, items, side),
+        grid=(wide // chunk,),
+        in_specs=[
+            pl.BlockSpec((tokens, channels), fixed),
+            pl.BlockSpec((rims, channels), fixed),
+            pl.BlockSpec((tokens, channels), fixed),
+            pl.BlockSpec((channels, chunk), columns),
+            pl.BlockSpec((chunk, channels), rows),
+            pl.BlockSpec((16, chunk), columns),
+        ],
+        out_specs=[
+            pl.BlockSpec((tokens, channels), fixed),
+            pl.BlockSpec((tokens, chunk), columns),
+            pl.BlockSpec((chunk, channels), rows),
+            pl.BlockSpec((16, chunk), columns),
+        ],
+        out_shape=[
+            jax.ShapeDtypeStruct((tokens, channels), jnp.float32),
+            jax.ShapeDtypeStruct((tokens, wide), jnp.bfloat16),
+            jax.ShapeDtypeStruct((wide, channels), jnp.bfloat16),
+            jax.ShapeDtypeStruct((16, wide), jnp.float32),
+        ],
+        scratch_shapes=[
+            pltpu.VMEM((items * (side + 2), side + 2 * INSET, chunk), jnp.float32),
+            pltpu.VMEM((rims, chunk), jnp.float32),
+            pltpu.VMEM((tokens, chunk), jnp.bfloat16),
+            pltpu.VMEM((tokens, chunk), jnp.float32),
+        ],
+        cost_estimate=pl.CostEstimate(
+            flops=8 * tokens * channels * wide,
+            bytes_accessed=4 * channels * wide * 4,
+            transcendentals=tokens * wide,
+        ),
+        name="ffn",
+    )(second, rim, d_two, w_up, w_down, taps)
+
+
+def ffn_back_pass(d_filtered, rim, flipped, w_up, taps, items, side, chunk=256):
+    tokens, wide = d_filtered.shape
+    channels = w_up.shape[0]
+    rims = rim.shape[0]
+    fixed = lambda step: (0, 0)
+    columns = lambda step: (0, step)
+    return pl.pallas_call(
+        functools.partial(ffn_back_kernel, items, side),
+        grid=(wide // chunk,),
+        in_specs=[
+            pl.BlockSpec((tokens, chunk), columns),
+            pl.BlockSpec((rims, chunk), columns),
+            pl.BlockSpec((channels, tokens), fixed),
+            pl.BlockSpec((channels, chunk), columns),
+            pl.BlockSpec((16, chunk), columns),
+        ],
+        out_specs=[
+            pl.BlockSpec((channels, chunk), columns),
+            pl.BlockSpec((tokens, channels), fixed),
+        ],
+        out_shape=[
+            jax.ShapeDtypeStruct((channels, wide), jnp.bfloat16),
+            jax.ShapeDtypeStruct((tokens, channels), jnp.float32),
+        ],
+        scratch_shapes=[
+            pltpu.VMEM((items * (side + 2), side + 2 * INSET, chunk), jnp.float32),
+            pltpu.VMEM((rims, chunk), jnp.float32),
+            pltpu.VMEM((tokens, chunk), jnp.bfloat16),
+        ],
+        cost_estimate=pl.CostEstimate(
+            flops=4 * tokens * channels * wide,
+            bytes_accessed=4 * channels * wide * 2,
+            transcendentals=0,
+        ),
+        name="ffn_back",
+    )(d_filtered, rim, flipped, w_up, taps)
+
+
 def shards(
     tokens, condition, counts, w_mod, w_qkv, w_out, w_up, w_down, conv_attn, conv_ffn, cotangent
 ):
@@ -211,33 +478,38 @@
     hidden_one = start_map + gate_a * branch
     second_f, pull_ffn_norm = jax.vjp(modulate, hidden_one, shift_f, scale_f)
     second = second_f.astype(jnp.bfloat16)
-    raised = jnp.dot(second, w_up, preferred_element_type=jnp.float32).astype(jnp.bfloat16)
-    padded_ffn = extend(raised, row_half, col_half, ffn_across, ffn_down)
-    filtered = apply_taps(padded_ffn, conv_ffn, half_side, False)
-    activated = gelu_tanh(filtered).astype(jnp.bfloat16)
-    branch_two = jnp.dot(activated, w_down, preferred_element_type=jnp.float32)
-    output = ((hidden_one + gate_f * branch_two) * living).astype(jnp.bfloat16)
+    token_count = item_count * quad_rows
     grad_res = (
         cotangent.reshape(item_count, half_side, half_side, channels).astype(jnp.float32) * living
     )
+    d_branch_two = (grad_res * gate_f).astype(jnp.bfloat16)
+    taps_ffn = jnp.pad(conv_ffn.astype(jnp.float32).T, ((0, 7), (0, 0)))
+    flat_second = second.reshape(token_count, channels)
+    branch_two, d_filtered, down_grad, tap_grad = ffn_pass(
+        flat_second,
+        rim_exchange(second, row_half, col_half).reshape(-1, channels),
+        d_branch_two.reshape(token_count, channels),
+        w_up,
+        w_down,
+        taps_ffn,
+        item_count,
+        half_side,
+    )
+    conv_ffn_grad = tap_grad[:9].T
+    branch_two = branch_two.reshape(start_map.shape)
+    output = ((hidden_one + gate_f * branch_two) * living).astype(jnp.bfloat16)
     d_gate_f = jnp.sum(grad_res * branch_two, (1, 2))
-    d_branch_two = (grad_res * gate_f).astype(jnp.bfloat16)
-    down_grad = jnp.einsum(
-        "ixyf,ixyd->fd", activated, d_branch_two, preferred_element_type=jnp.float32
-    )
-    d_activated = jnp.einsum(
-        "ixyd,fd->ixyf", d_branch_two, w_down, preferred_element_type=jnp.float32
-    )
-    again = jnp.dot(second, w_up, preferred_element_type=jnp.float32).astype(jnp.bfloat16)
-    kept_pad = extend(again, row_half, col_half, ffn_across, ffn_down)
-    kept_filter = apply_taps(kept_pad, conv_ffn, half_side, False)
-    _, gelu_pull = jax.vjp(gelu_tanh, kept_filter)
-    d_filtered = gelu_pull(d_activated)[0].astype(jnp.bfloat16)
-    conv_ffn_grad = tap_grads(kept_pad, d_filtered, half_side)
-    d_padded_ffn = extend(d_filtered, row_half, col_half, ffn_across, ffn_down)
-    d_raised = apply_taps(d_padded_ffn, conv_ffn, half_side, True).astype(jnp.bfloat16)
-    up_grad = jnp.einsum("ixyd,ixyf->df", second, d_raised, preferred_element_type=jnp.float32)
-    d_second = jnp.einsum("ixyf,df->ixyd", d_raised, w_up, preferred_element_type=jnp.float32)
+    d_filtered_map = d_filtered.reshape(item_count, half_side, half_side, -1)
+    up_grad, d_second = ffn_back_pass(
+        d_filtered,
+        rim_exchange(d_filtered_map, row_half, col_half).reshape(-1, w_up.shape[1]),
+        flat_second.T,
+        w_up,
+        taps_ffn,
+        item_count,
+        half_side,
+    )
+    d_second = d_second.reshape(start_map.shape)
     d_hidden_part, d_shift_f, d_scale_f = pull_ffn_norm(d_second)
     d_hidden = grad_res + d_hidden_part
     d_gate_a = jnp.sum(d_hidden * branch, (1, 2))

time: 608 us -> 638 us (1.049)
  Pallas kernels: 0 us -> 126 us
  matrix products: 145 us -> 72.6 us
  other arithmetic: 158 us -> 120 us
  local copies, waits for them, and re-layouts: 151 us -> 167 us
  waiting for transfers between devices: 91.6 us -> 79.1 us
  starting transfers between devices: 49.7 us -> 59.5 us
    pallas_call x0 -> x2, Pallas kernels: none -> 126 us  [the longest x1 83.1 us: ffn_pass(): pl.pallas_call(functools.partial(ffn_kernel, items, side), grid=(wide //...]
    dot_general x6 -> x0, matrix products: 74.6 us -> none  [the longest x1 35.1 us: shards(): jnp.einsum('ixyd,fd->ixyf', d_branch_two, w_down, preferred_element_type=...]
    concatenate x4 -> x2, other arithmetic: 27.2 us -> 2.52 us  [extend(): return jnp.concatenate([top_rim, widened, bottom_rim], 1)]
    concatenate x0 -> x2, local copies, waits for them, and re-layouts: none -> 20 us  [rim_exchange(): jnp.concatenate([kept(column, left), kept(column, ~left), kept(row, upper...]
    select_n x0 -> x12, other arithmetic: none -> 16.7 us  [the longest x6 9.61 us: kept(): return jnp.where(where, values, jnp.zeros_like(values))]
    ppermute x36 -> x32, waiting for transfers between devices: 69.2 us -> 52.7 us  [from_partner(): lax.ppermute(shard, axis, [(i, i ^ 1 << bit) for i in range(lax.axis_size...]
    add x1 -> x0, other arithmetic: 15.6 us -> none  [apply_taps(): summed = summed + window * weights_f[:, stencil]]
    another operation x22 -> x11, local copies, waits for them, and re-layouts: 19.4 us -> 8.97 us  [tap_grads(): return jnp.stack(columns, 1)]
  transfers between devices with their start and end apart: 40 -> 42, of which waited for: 22 -> 19; matrix products, arithmetic and copies ran while one was open for 55% -> 46% of each run, Pallas kernels for 0% -> 7%
where the time goes in v2:
time: 638 us; the launch traced here: 627 us
  local copies, waits for them, and re-layouts  167 us (26%)
  Pallas kernels  126 us (20%)
  other arithmetic  120 us (19%)
  waiting for transfers between devices  79.1 us (12%)
  matrix products  72.6 us (11%)
  starting transfers between devices  59.5 us (9%)
    pallas_call x1, Pallas kernels, ffn_pass(): pl.pallas_call(functools.partial(ffn_kernel, items, side), grid=(wide //...  83.1 us
    ppermute x32, waiting for transfers between devices, from_partner(): lax.ppermute(shard, axis, [(i, i ^ 1 << bit) for i in range(lax.axis_size...  52.7 us
    pallas_call x1, Pallas kernels, ffn_back_pass(): pl.pallas_call(functools.partial(ffn_back_kernel, items, side), grid=(wid...  42.5 us
    ppermute x32, starting transfers between devices, from_partner(): lax.ppermute(shard, axis, [(i, i ^ 1 << bit) for i in range(lax.axis_size...  37 us
    unnamed x192, local copies, waits for them, and re-layouts  21.2 us
    concatenate x2, local copies, waits for them, and re-layouts, rim_exchange(): jnp.concatenate([kept(column, left), kept(column, ~left), kept(row, upper...  20 us
    all_to_all x2, waiting for transfers between devices, to_groups(): lax.all_to_all(pieces, 'narrow', split_axis=1, concat_axis=1, tiled=True)  16.5 us
    convert_element_type x16, other arithmetic, halving_sum(): held = held.astype(jnp.bfloat16)  15.2 us
  transfers between devices with their start and end apart: 42, of which 19 were waited for; matrix products, arithmetic and copies ran while one was open for 46% of the time, Pallas kernels for 7%

profile of v2, /device:TPU:0, one launch (start us, length us, event | category | flops | bytes accessed | tf_op | source)
XLA Modules:
  0.0 627.3 jit_solution(17102576148787090699)
XLA Ops:
  10.2 4.7 fusion.104
  33.2 4.7 collective-permute-done.1
  51.6 4.8 all-to-all-start
  63.6 8.8 %all-to-all-done = bf16[3,4,64,768]{3,2,0,1:T(8,128)(2,1)} async-done(((bf16[3,4,64,768]{3,2,0,1:T(8,128)(2,1)}), bf16[3,4,64,768]{3,2,0,1:T(8,128)(2,1)}, u32[]{:S(2)}, u32[]{:S(2)}) %all-to-all-start) | async-done | bytes 1179680 | tf_op jit(solution)/shard_map/all_to_all | solution.py:90
  74.7 4.3 convolution_convert_fusion
  79.1 5.7 copy.138
  92.2 4.6 fusion.53
  96.8 4.6 reshape_reshape.12
  101.4 5.1 copy.143
  106.4 4.4 all-to-all-start.1
  134.0 4.9 fusion.99
  153.7 7.6 %concatenate.86 = bf16[3,72,768]{2,1,0:T(8,128)(2,1)} concatenate(bf16[3,16,768]{2,1,0:T(8,128)(2,1)} %get-tuple-element.138, bf16[3,16,768]{2,1,0:T(8,128)(2,1)} %get-tuple-element.137, bf16[3,16,768]{2,1,0:T(8,128)(2,1)} %get-tuple-element.136, bf16[3,16,768]{2,1,0:T(8,128)(2,1)} %get-tuple-element.135, bf16[3,1,768]{2,1,0:T(2,128)(2,1)} %get-tuple-element.154, ...), dimensions={1} | concatenate | bytes 663552 | tf_op jit(solution)/shard_map/concatenate | solution.py:187
  161.2 83.1 %ffn.1 = (f32[768,768]{1,0:T(8,128)}, bf16[768,3072]{1,0:T(8,128)(2,1)}, bf16[3072,768]{1,0:T(8,128)(2,1)}, f32[16,3072]{1,0:T(8,128)}) custom-call(bf16[768,768]{1,0:T(8,128)(2,1)} %bitcast.317, bf16[216,768]{1,0:T(8,128)(2,1)} %bitcast.342, bf16[768,768]{1,0:T(8,128)(2,1)} %fusion.43.d_two_ref, bf16[768,3072]{1,0:T(8,128)(2,1)} %w_up_ref.3, ...), custom_call_target="tpu_custom_call" | custom-call | flops 14495514624 | bytes 37748736 | tf_op jit(solution)/shard_map/ffn/pallas_call | solution.py:366
  274.9 12.5 %concatenate.87 = bf16[3,72,3072]{2,1,0:T(8,128)(2,1)} concatenate(bf16[3,16,3072]{2,1,0:T(8,128)(2,1)} %get-tuple-element.118, bf16[3,16,3072]{2,1,0:T(8,128)(2,1)} %get-tuple-element.117, bf16[3,16,3072]{2,1,0:T(8,128)(2,1)} %get-tuple-element.116, bf16[3,16,3072]{2,1,0:T(8,128)(2,1)} %get-tuple-element.115, bf16[3,1,3072]{2,1,0:T(2,128)(2,1)} %get-tuple-element.146, ...), dimensions={1} | concatenate | bytes 2654208 | tf_op jit(solution)/shard_map/concatenate | solution.py:187
  287.3 42.5 %ffn_back.1 = (bf16[768,3072]{1,0:T(8,128)(2,1)}, f32[768,768]{1,0:T(8,128)}) custom-call(bf16[768,3072]{1,0:T(8,128)(2,1)} %get-tuple-element.17.d_filtered_ref, bf16[216,3072]{1,0:T(8,128)(2,1)} %bitcast.330, bf16[768,768]{1,0:T(8,128)(2,1)} %bitcast.336, bf16[768,3072]{1,0:T(8,128)(2,1)} %w_up_ref.3, f32[16,3072]{1,0:T(8,128)} %pad_convert_fusion.taps_ref), custom_call_target="tpu_custom_call" | custom-call | flops 7247757312 | bytes 18874368 | tf_op jit(solution)/shard_map/ffn_back/pallas_call | solution.py:410
  353.2 4.7 all-to-all-start.2
  366.1 7.8 %all-to-all-done.2 = bf16[3,4,64,768]{3,2,0,1:T(8,128)(2,1)} async-done(((bf16[3,4,64,768]{3,2,0,1:T(8,128)(2,1)}), bf16[3,4,64,768]{3,2,0,1:T(8,128)(2,1)}, u32[]{:S(2)}, u32[]{:S(2)}) %all-to-all-start.2) | async-done | bytes 1179680 | tf_op jit(solution)/shard_map/all_to_all | solution.py:90
  373.8 5.2 copy.155
  379.0 4.5 reshape_reshape.13
  383.5 10.8 %multiply_reduce_fusion = (f32[3,12,256]{2,1,0:T(8,128)}, f32[3,12,256,256]{2,3,1,0:T(8,128)}) fusion(f32[3,12,256,256]{2,3,1,0:T(8,128)} %copy-done.1, f32[3,12,256]{2,1,0:T(8,128)} %log_add_fusion, bf16[3,256,12,64]{1,3,2,0:T(8,128)(2,1)} %reshape_reshape.13, bf16[3,256,3,12,64]{1,4,3,2,0:T(8,128)(2,1)} %bitcast.306), kind=kOutput, calls=%fused_computation.1 | convolution fusion | flops 311417856 | bytes 21319680 | tf_op jit(solution)/shard_map/iqhe,ikhe->ihqk/dot_general | solution.py:526
  394.3 11.4 %multiply_convert_fusion = bf16[3,12,256,256]{2,3,1,0:T(8,128)(2,1)} fusion(f32[3,12,256,256]{2,3,1,0:T(8,128)} %get-tuple-element.161, f32[3,12,256,256]{2,3,1,0:T(8,128)} %copy-done.1, f32[3,12,256]{2,1,0:T(8,128)} %get-tuple-element.160, f32[3,12,256]{2,1,0:T(8,128)} %log_add_fusion), kind=kLoop, calls=%fused_computation | loop fusion | flops 11796480 | bytes 23666688 | tf_op jit(solution)/shard_map/convert_element_type | solution.py:530
  412.7 5.5 fusion.46
  427.6 5.3 bitcast_convert_fusion
  435.9 7.6 %all-to-all-done.3 = bf16[3,4,64,768]{3,2,0,1:T(8,128)(2,1)} async-done(((bf16[3,4,64,768]{3,2,0,1:T(8,128)(2,1)}), bf16[3,4,64,768]{3,2,0,1:T(8,128)(2,1)}, u32[]{:S(2)}, u32[]{:S(2)}) %all-to-all-start.3) | async-done | bytes 1179680 | tf_op jit(solution)/shard_map/all_to_all | solution.py:97
  450.8 6.3 %fusion.39 = (bf16[768]{0:T(1024)(128)(2,1)S(1)}, bf16[768]{0:T(1024)(128)(2,1)S(1)}, bf16[768]{0:T(1024)(128)(2,1)S(1)}, bf16[768]{0:T(1024)(128)(2,1)S(1)}, bf...) fusion(bf16[3,16,16,768]{3,1,0,2:T(8,128)(2,1)} %reshape.348, ...), kind=kLoop, calls=%fused_computation.74 | loop fusion | flops 18278400 | bytes 9596928 | tf_op jit(solution)/shard_map/reduce_sum | solution.py:81
  467.4 4.3 reshape.372
  510.0 4.9 fusion.84
  514.9 5.7 fusion.93
  540.5 7.1 %collective-permute-done.17 = f32[4,3,4608]{2,1,0:T(4,128)S(1)} collective-permute-done((f32[4,3,4608]{2,1,0:T(4,128)S(1)}, f32[4,3,4608]{2,1,0:T(4,128)S(1)}, u32[]{:S(2)}, u32[]{:S(2)}) %collective-permute-start.17) | collective-permute-done | bytes 221216 | tf_op jit(solution)/shard_map/ppermute | solution.py:19
  556.9 6.7 %collective-permute-done.20 = bf16[2,2,24,1536]{3,2,1,0:T(8,128)(2,1)S(1)} collective-permute-done((bf16[2,2,24,1536]{3,2,1,0:T(8,128)(2,1)S(1)}, bf16[2,2,24,1536]{3,2,1,0:T(8,128)(2,1)S(1)}, u32[]{:S(2)}, u32[]{:S(2)}) %collective-permute-start.20) | collective-permute-done | bytes 294944 | tf_op jit(solution)/shard_map/ppermute | solution.py:19
  581.6 8.3 %collective-permute-done.24 = bf16[2,2,2,24,1664]{4,3,0,1,2:T(8,128)(2,1)S(1)} collective-permute-done((bf16[2,2,2,24,1664]{4,3,0,1,2:T(8,128)(2,1)S(1)}, bf16[2,2,2,24,1664]{4,3,0,1,2:T(8,128)(2,1)S(1)}, u32[]{:S(2)}, u32[]{:S(2)}) %collective-permute-start.24) | collective-permute-done | bytes 639008 | tf_op jit(solution)/shard_map/ppermute | solution.py:19
  601.2 5.3 collective-permute-done.26
  (445 shorter events, 310.7 us)
Async XLA Ops:
  25.7 34.3 %collective-permute-start.12 = (bf16[1,3,768]{2,1,0:T(4,128)(2,1)}, bf16[1,3,768]{2,1,0:T(4,128)(2,1)}, u32[]{:S(2)}, u32[]{:S(2)}) collective-permute-start(bf16[1,3,768]{2,1,0:T(4,128)(2,1)} %fusion.119), channel_id=1, source_target_pairs={{0,4},{4,0},{8,12},{12,8},{16,20},{20,16},{24,28},{28,24},{1,5},{5... | collective-permute-start | bytes 13832 | tf_op jit(solution)/shard_map/ppermute | solution.py:19
  31.5 6.4 %collective-permute-start.1 = (bf16[3,1,18,768]{3,1,0,2:T(2,128)(2,1)S(1)}, bf16[3,1,18,768]{3,1,0,2:T(2,128)(2,1)S(1)}, u32[]{:S(2)}, u32[]{:S(2)}) collective-permute-start(bf16[3,1,18,768]{3,1,0,2:T(2,128)(2,1)S(1)} %broadcast_select_fusion.3), channel_id=1, source_target_pairs={{0,2},{1,3},{2,0},{3,1},{4,6},{5,7},{6,4},{7,5},{8,10},{9,11},{10,... | collective-permute-start | bytes 248840 | tf_op jit(solution)/shard_map/ppermute | solution.py:19
  51.6 20.7 %all-to-all-start = ((bf16[3,4,64,768]{3,2,0,1:T(8,128)(2,1)}), bf16[3,4,64,768]{3,2,0,1:T(8,128)(2,1)}, u32[]{:S(2)}, u32[]{:S(2)}) async-start(bf16[3,4,64,768]{3,2,0,1:T(8,128)(2,1)} %bitcast.322), calls=%async_computation | async-start | bytes 2359296 | tf_op jit(solution)/shard_map/all_to_all | solution.py:90
  62.0 48.9 %collective-permute-start.13 = (bf16[2,3,768]{2,1,0:T(4,128)(2,1)}, bf16[2,3,768]{2,1,0:T(4,128)(2,1)}, u32[]{:S(2)}, u32[]{:S(2)}) collective-permute-start(bf16[2,3,768]{2,1,0:T(4,128)(2,1)} %pad_maximum_fusion.17), channel_id=1, source_target_pairs={{0,8},{4,12},{8,0},{12,4},{16,24},{20,28},{24,16},{28,20},{1,9},{5... | collective-permute-start | bytes 27656 | tf_op jit(solution)/shard_map/ppermute | solution.py:19
  106.4 20.3 %all-to-all-start.1 = ((bf16[3,4,64,768]{3,2,0,1:T(8,128)(2,1)}), bf16[3,4,64,768]{3,2,0,1:T(8,128)(2,1)}, u32[]{:S(2)}, u32[]{:S(2)}) async-start(bf16[3,4,64,768]{3,2,0,1:T(8,128)(2,1)} %copy.143), calls=%async_computation.1 | async-start | bytes 2359296 | tf_op jit(solution)/shard_map/all_to_all | solution.py:97
  112.9 7.3 %collective-permute-start.14 = (bf16[4,3,768]{2,1,0:T(4,128)(2,1)}, bf16[4,3,768]{2,1,0:T(4,128)(2,1)}, u32[]{:S(2)}, u32[]{:S(2)}) collective-permute-start(bf16[4,3,768]{2,1,0:T(4,128)(2,1)} %pad_maximum_fusion.16), channel_id=1, source_target_pairs={{0,16},{4,20},{8,24},{12,28},{16,0},{20,4},{24,8},{28,12},{1,17},{... | collective-permute-start | bytes 55304 | tf_op jit(solution)/shard_map/ppermute | solution.py:19
  143.4 8.1 %collective-permute-start.3 = (bf16[3,16,768]{2,1,0:T(8,128)(2,1)}, bf16[3,16,768]{2,1,0:T(8,128)(2,1)}, u32[]{:S(2)}, u32[]{:S(2)}) collective-permute-start(bf16[3,16,768]{2,1,0:T(8,128)(2,1)} %fusion.82), channel_id=1, source_target_pairs={{0,2},{1,3},{2,0},{3,1},{4,6},{5,7},{6,4},{7,5},{8,10},{9,11},{10,... | collective-permute-start | bytes 221192 | tf_op jit(solution)/shard_map/ppermute | solution.py:178
  249.4 23.0 %collective-permute-start.6 = (bf16[3,16,3072]{2,1,0:T(8,128)(2,1)}, bf16[3,16,3072]{2,1,0:T(8,128)(2,1)}, u32[]{:S(2)}, u32[]{:S(2)}) collective-permute-start(bf16[3,16,3072]{2,1,0:T(8,128)(2,1)} %fusion.73), channel_id=1, source_target_pairs={{0,2},{1,3},{2,0},{3,1},{4,6},{5,7},{6,4},{7,5},{8,10},{9,11},{10,... | collective-permute-start | bytes 884744 | tf_op jit(solution)/shard_map/ppermute | solution.py:178
  257.2 267.9 %collective-permute-start.33 = (bf16[2,2,2,2,96,768]{5,4,0,1,2,3:T(8,128)(2,1)}, bf16[2,2,2,2,96,768]{5,4,0,1,2,3:T(8,128)(2,1)}, u32[]{:S(2)}, u32[]{:S(2)}) collective-permute-start(bf16[2,2,2,2,96,768]{5,4,0,1,2,3:T(8,128)(2,1)} %bitcast.295), channel_id=1, source_target_pairs={{0,1},{1,0},{2,3},{3,2},{4,5},{5,4},{6,7},{7,6},{8,9},{9,8},{10,11... | collective-permute-start | bytes 7077896 | tf_op jit(solution)/shard_map/ppermute | solution.py:19
  258.1 12.5 %collective-permute-start.5 = (bf16[3,16,3072]{2,1,0:T(8,128)(2,1)}, bf16[3,16,3072]{2,1,0:T(8,128)(2,1)}, u32[]{:S(2)}, u32[]{:S(2)}) collective-permute-start(bf16[3,16,3072]{2,1,0:T(8,128)(2,1)} %fusion.74), channel_id=1, source_target_pairs={{0,1},{1,0},{2,3},{3,2},{4,5},{5,4},{6,7},{7,6},{8,9},{9,8},{10,11... | collective-permute-start | bytes 884744 | tf_op jit(solution)/shard_map/ppermute | solution.py:177
  258.6 10.4 %collective-permute-start.7 = (bf16[3,1,3072]{2,1,0:T(2,128)(2,1)}, bf16[3,1,3072]{2,1,0:T(2,128)(2,1)}, u32[]{:S(2)}, u32[]{:S(2)}) collective-permute-start(bf16[3,1,3072]{2,1,0:T(2,128)(2,1)} %broadcast_select_fusion.17), channel_id=1, source_target_pairs={{0,3},{1,2},{2,1},{3,0},{4,7},{5,6},{6,5},{7,4},{8,11},{9,10},{10,... | collective-permute-start | bytes 55304 | tf_op jit(solution)/shard_map/ppermute | solution.py:179
  335.7 200.0 %collective-permute-start.28 = (bf16[2,2,2,2,24,3072]{5,4,0,1,3,2:T(8,128)(2,1)}, bf16[2,2,2,2,24,3072]{5,4,0,1,3,2:T(8,128)(2,1)}, u32[]{:S(2)}, u32[]{:S(2)}) collective-permute-start(bf16[2,2,2,2,24,3072]{5,4,0,1,3,2:T(8,128)(2,1)} %bitcast.296), channel_id=1, source_target_pairs={{0,1},{1,0},{2,3},{3,2},{4,5},{5,4},{6,7},{7,6},{8,9},{9,8},{10,11... | collective-permute-start | bytes 7077896 | tf_op jit(solution)/shard_map/ppermute | solution.py:19
  353.2 20.6 %all-to-all-start.2 = ((bf16[3,4,64,768]{3,2,0,1:T(8,128)(2,1)}), bf16[3,4,64,768]{3,2,0,1:T(8,128)(2,1)}, u32[]{:S(2)}, u32[]{:S(2)}) async-start(bf16[3,4,64,768]{3,2,0,1:T(8,128)(2,1)} %bitcast.323), calls=%async_computation.2 | async-start | bytes 2359296 | tf_op jit(solution)/shard_map/all_to_all | solution.py:90
  423.3 20.2 %all-to-all-start.3 = ((bf16[3,4,64,768]{3,2,0,1:T(8,128)(2,1)}), bf16[3,4,64,768]{3,2,0,1:T(8,128)(2,1)}, u32[]{:S(2)}, u32[]{:S(2)}) async-start(bf16[3,4,64,768]{3,2,0,1:T(8,128)(2,1)} %copy.161), calls=%async_computation.3 | async-start | bytes 2359296 | tf_op jit(solution)/shard_map/all_to_all | solution.py:97
  435.5 85.2 %collective-permute-start.18 = (bf16[2,2,2,2,24,1536]{5,4,3,2,1,0:T(8,128)(2,1)}, bf16[2,2,2,2,24,1536]{5,4,3,2,1,0:T(8,128)(2,1)}, u32[]{:S(2)}, u32[]{:S(2)}) collective-permute-start(bf16[2,2,2,2,24,1536]{5,4,3,2,1,0:T(8,128)(2,1)} %dynamic-slice_bitcast_fusion.2), channel_id=1, source_target_pairs={{0,1},{1,0},{2,3},{3,2},{4,5},{5,4},{6,7},{7,6},{8,9},{9,8},{10,11... | collective-permute-start | bytes 3538952 | tf_op jit(solution)/shard_map/ppermute | solution.py:19
  483.6 6.7 %collective-permute-start.9 = (bf16[3,1,18,768]{3,1,0,2:T(2,128)(2,1)S(1)}, bf16[3,1,18,768]{3,1,0,2:T(2,128)(2,1)S(1)}, u32[]{:S(2)}, u32[]{:S(2)}) collective-permute-start(bf16[3,1,18,768]{3,1,0,2:T(2,128)(2,1)S(1)} %broadcast_select_fusion.1), channel_id=1, source_target_pairs={{0,2},{1,3},{2,0},{3,1},{4,6},{5,7},{6,4},{7,5},{8,10},{9,11},{10,... | collective-permute-start | bytes 248840 | tf_op jit(solution)/shard_map/ppermute | solution.py:19
  486.5 77.8 %collective-permute-start.23 = (bf16[2,2,2,2,24,1664]{5,4,0,1,2,3:T(8,128)(2,1)}, bf16[2,2,2,2,24,1664]{5,4,0,1,2,3:T(8,128)(2,1)}, u32[]{:S(2)}, u32[]{:S(2)}) collective-permute-start(bf16[2,2,2,2,24,1664]{5,4,0,1,2,3:T(8,128)(2,1)} %bitcast.297), channel_id=1, source_target_pairs={{0,1},{1,0},{2,3},{3,2},{4,5},{5,4},{6,7},{7,6},{8,9},{9,8},{10,11... | collective-permute-start | bytes 3833864 | tf_op jit(solution)/shard_map/ppermute | solution.py:19
  509.7 17.9 %collective-permute-start.15 = (f32[1,3,4608]{2,1,0:T(4,128)S(1)}, f32[1,3,4608]{2,1,0:T(4,128)S(1)}, u32[]{:S(2)}, u32[]{:S(2)}) collective-permute-start(f32[1,3,4608]{2,1,0:T(4,128)S(1)} %bitcast.331), channel_id=1, source_target_pairs={{0,4},{4,0},{8,12},{12,8},{16,20},{20,16},{24,28},{28,24},{1,5},{5... | collective-permute-start | bytes 165896 | tf_op jit(solution)/shard_map/ppermute | solution.py:19
  523.4 27.2 %collective-permute-start.19 = (bf16[2,2,2,24,1536]{4,3,2,1,0:T(8,128)(2,1)}, bf16[2,2,2,24,1536]{4,3,2,1,0:T(8,128)(2,1)}, u32[]{:S(2)}, u32[]{:S(2)}) collective-permute-start(bf16[2,2,2,24,1536]{4,3,2,1,0:T(8,128)(2,1)} %dynamic-slice_bitcast_fusion.6), channel_id=1, source_target_pairs={{0,4},{4,0},{8,12},{12,8},{16,20},{20,16},{24,28},{28,24},{1,5},{5... | collective-permute-start | bytes 1769480 | tf_op jit(solution)/shard_map/ppermute | solution.py:19
  530.4 45.3 %collective-permute-start.34 = (bf16[2,2,2,96,768]{4,3,0,1,2:T(8,128)(2,1)}, bf16[2,2,2,96,768]{4,3,0,1,2:T(8,128)(2,1)}, u32[]{:S(2)}, u32[]{:S(2)}) collective-permute-start(bf16[2,2,2,96,768]{4,3,0,1,2:T(8,128)(2,1)} %dynamic-slice_bitcast_fusion), channel_id=1, source_target_pairs={{0,2},{1,3},{2,0},{3,1},{4,6},{5,7},{6,4},{7,5},{8,10},{9,11},{10,... | collective-permute-start | bytes 3538952 | tf_op jit(solution)/shard_map/ppermute | solution.py:19
  533.0 14.6 %collective-permute-start.17 = (f32[4,3,4608]{2,1,0:T(4,128)S(1)}, f32[4,3,4608]{2,1,0:T(4,128)S(1)}, u32[]{:S(2)}, u32[]{:S(2)}) collective-permute-start(f32[4,3,4608]{2,1,0:T(4,128)S(1)} %pad_maximum_fusion.8), channel_id=1, source_target_pairs={{0,16},{4,20},{8,24},{12,28},{16,0},{20,4},{24,8},{28,12},{1,17},{... | collective-permute-start | bytes 663560 | tf_op jit(solution)/shard_map/ppermute | solution.py:19
  539.9 38.2 %collective-permute-start.29 = (bf16[2,2,2,24,3072]{4,3,0,1,2:T(8,128)(2,1)}, bf16[2,2,2,24,3072]{4,3,0,1,2:T(8,128)(2,1)}, u32[]{:S(2)}, u32[]{:S(2)}) collective-permute-start(bf16[2,2,2,24,3072]{4,3,0,1,2:T(8,128)(2,1)} %dynamic-slice_bitcast_fusion.1), channel_id=1, source_target_pairs={{0,4},{4,0},{8,12},{12,8},{16,20},{20,16},{24,28},{28,24},{1,5},{5... | collective-permute-start | bytes 3538952 | tf_op jit(solution)/shard_map/ppermute | solution.py:19
  552.1 11.5 %collective-permute-start.20 = (bf16[2,2,24,1536]{3,2,1,0:T(8,128)(2,1)S(1)}, bf16[2,2,24,1536]{3,2,1,0:T(8,128)(2,1)S(1)}, u32[]{:S(2)}, u32[]{:S(2)}) collective-permute-start(bf16[2,2,24,1536]{3,2,1,0:T(8,128)(2,1)S(1)} %dynamic-slice_bitcast_fusion.10), channel_id=1, source_target_pairs={{0,2},{1,3},{2,0},{3,1},{4,6},{5,7},{6,4},{7,5},{8,10},{9,11},{10,... | collective-permute-start | bytes 884744 | tf_op jit(solution)/shard_map/ppermute | solution.py:19
  572.5 17.3 %collective-permute-start.24 = (bf16[2,2,2,24,1664]{4,3,0,1,2:T(8,128)(2,1)S(1)}, bf16[2,2,2,24,1664]{4,3,0,1,2:T(8,128)(2,1)S(1)}, u32[]{:S(2)}, u32[]{:S(2)}) collective-permute-start(bf16[2,2,2,24,1664]{4,3,0,1,2:T(8,128)(2,1)S(1)} %dynamic-slice_bitcast_fusion.3), channel_id=1, source_target_pairs={{0,2},{1,3},{2,0},{3,1},{4,6},{5,7},{6,4},{7,5},{8,10},{9,11},{10,... | collective-permute-start | bytes 1916936 | tf_op jit(solution)/shard_map/ppermute | solution.py:19
  577.5 14.8 %collective-permute-start.35 = (bf16[2,2,96,768]{3,2,0,1:T(8,128)(2,1)S(1)}, bf16[2,2,96,768]{3,2,0,1:T(8,128)(2,1)S(1)}, u32[]{:S(2)}, u32[]{:S(2)}) collective-permute-start(bf16[2,2,96,768]{3,2,0,1:T(8,128)(2,1)S(1)} %dynamic-slice_bitcast_fusion.4), channel_id=1, source_target_pairs={{0,4},{4,0},{8,12},{12,8},{16,20},{20,16},{24,28},{28,24},{1,5},{5... | collective-permute-start | bytes 1769480 | tf_op jit(solution)/shard_map/ppermute | solution.py:19
  579.9 17.9 %collective-permute-start.30 = (bf16[2,2,24,3072]{3,2,0,1:T(8,128)(2,1)S(1)}, bf16[2,2,24,3072]{3,2,0,1:T(8,128)(2,1)S(1)}, u32[]{:S(2)}, u32[]{:S(2)}) collective-permute-start(bf16[2,2,24,3072]{3,2,0,1:T(8,128)(2,1)S(1)} %dynamic-slice_bitcast_fusion.5), channel_id=1, source_target_pairs={{0,2},{1,3},{2,0},{3,1},{4,6},{5,7},{6,4},{7,5},{8,10},{9,11},{10,... | collective-permute-start | bytes 1769480 | tf_op jit(solution)/shard_map/ppermute | solution.py:19
  590.1 7.1 %collective-permute-start.25 = (bf16[2,2,24,1664]{3,2,0,1:T(8,128)(2,1)S(1)}, bf16[2,2,24,1664]{3,2,0,1:T(8,128)(2,1)S(1)}, u32[]{:S(2)}, u32[]{:S(2)}) collective-permute-start(bf16[2,2,24,1664]{3,2,0,1:T(8,128)(2,1)S(1)} %dynamic-slice_bitcast_fusion.7), channel_id=1, source_target_pairs={{0,4},{4,0},{8,12},{12,8},{16,20},{20,16},{24,28},{28,24},{1,5},{5... | collective-permute-start | bytes 958472 | tf_op jit(solution)/shard_map/ppermute | solution.py:19
  592.5 8.6 %collective-permute-start.36 = (bf16[2,96,768]{2,1,0:T(8,128)(2,1)S(1)}, bf16[2,96,768]{2,1,0:T(8,128)(2,1)S(1)}, u32[]{:S(2)}, u32[]{:S(2)}) collective-permute-start(bf16[2,96,768]{2,1,0:T(8,128)(2,1)S(1)} %dynamic-slice_bitcast_fusion.8), channel_id=1, source_target_pairs={{0,8},{4,12},{8,0},{12,4},{16,24},{20,28},{24,16},{28,20},{1,9},{5... | collective-permute-start | bytes 884744 | tf_op jit(solution)/shard_map/ppermute | solution.py:19
  597.2 9.2 %collective-permute-start.26 = (bf16[2,24,1664]{2,1,0:T(8,128)(2,1)S(1)}, bf16[2,24,1664]{2,1,0:T(8,128)(2,1)S(1)}, u32[]{:S(2)}, u32[]{:S(2)}) collective-permute-start(bf16[2,24,1664]{2,1,0:T(8,128)(2,1)S(1)} %dynamic-slice_bitcast_fusion.11), channel_id=1, source_target_pairs={{0,8},{4,12},{8,0},{12,4},{16,24},{20,28},{24,16},{28,20},{1,9},{5... | collective-permute-start | bytes 479240 | tf_op jit(solution)/shard_map/ppermute | solution.py:19
  599.6 17.8 %collective-permute-start.31 = (bf16[2,24,3072]{2,1,0:T(8,128)(2,1)}, bf16[2,24,3072]{2,1,0:T(8,128)(2,1)}, u32[]{:S(2)}, u32[]{:S(2)}) collective-permute-start(bf16[2,24,3072]{2,1,0:T(8,128)(2,1)} %dynamic-slice_bitcast_fusion.9), channel_id=1, source_target_pairs={{0,8},{4,12},{8,0},{12,4},{16,24},{20,28},{24,16},{28,20},{1,9},{5... | collective-permute-start | bytes 884744 | tf_op jit(solution)/shard_map/ppermute | solution.py:19
  609.2 11.3 %collective-permute-start.37 = (bf16[96,768]{1,0:T(8,128)(2,1)}, bf16[96,768]{1,0:T(8,128)(2,1)}, u32[]{:S(2)}, u32[]{:S(2)}) collective-permute-start(bf16[96,768]{1,0:T(8,128)(2,1)} %dynamic-slice_bitcast_fusion.12), channel_id=1, source_target_pairs={{0,16},{4,20},{8,24},{12,28},{16,0},{20,4},{24,8},{28,12},{1,17},{... | collective-permute-start | bytes 442376 | tf_op jit(solution)/shard_map/ppermute | solution.py:19
  618.5 7.7 %collective-permute-start.32 = (bf16[24,3072]{1,0:T(8,128)(2,1)S(1)}, bf16[24,3072]{1,0:T(8,128)(2,1)S(1)}, u32[]{:S(2)}, u32[]{:S(2)}) collective-permute-start(bf16[24,3072]{1,0:T(8,128)(2,1)S(1)} %dynamic-slice_bitcast_fusion.13), channel_id=1, source_target_pairs={{0,16},{4,20},{8,24},{12,28},{16,0},{20,4},{24,8},{28,12},{1,17},{... | collective-permute-start | bytes 442376 | tf_op jit(solution)/shard_map/ppermute | solution.py:19
  (102 other events, 470.4 us)

commit v3 on v2

--- a/solution.py
+++ b/solution.py
@@ -164,69 +164,129 @@
 
 
 LANES = 128
-INSET = 8
+SUBLANES = 8
+UNROLL = 4
 GELU_SCALE = math.sqrt(2.0 / math.pi)
 GELU_CUBE = 0.044715
 
 
-def rim_exchange(field_map, row_half, col_half):
-    column = jnp.where(col_half == 0, field_map[:, :, -1], field_map[:, :, 0])
-    row = jnp.where(row_half == 0, field_map[:, -1], field_map[:, 0])
-    point = jnp.where(col_half == 0, row[:, -1:], row[:, :1])
+def send_rims(column, row, point):
     size = lax.axis_size("narrow")
     column = lax.ppermute(column, "narrow", [(i, i ^ 1) for i in range(size)])
     row = lax.ppermute(row, "narrow", [(i, i ^ 2) for i in range(size)])
     point = lax.ppermute(point, "narrow", [(i, i ^ 3) for i in range(size)])
-    upper = row_half == 1
-    left = col_half == 1
-
-    def kept(values, where):
-        return jnp.where(where, values, jnp.zeros_like(values))
-
-    spare = jnp.zeros((point.shape[0], 4) + point.shape[2:], point.dtype)
-    return jnp.concatenate(
-        [
-            kept(column, left),
-            kept(column, ~left),
-            kept(row, upper),
-            kept(row, ~upper),
-            kept(point, upper & left),
-            kept(point, upper & ~left),
-            kept(point, ~upper & left),
-            kept(point, ~upper & ~left),
-            spare,
-        ],
-        1,
-    )
-
-
-def fill_padded(padded, inner, rim, items, side):
+    channels = column.shape[-1]
+    point = jnp.pad(point, ((0, 8 - point.shape[0]), (0, 0)))
+    return column.reshape(-1, channels), row.reshape(-1, channels), point
+
+
+def map_rims(field_map, row_half, col_half):
+    items, side, _, channels = field_map.shape
+    column = jnp.where(col_half == 0, field_map[:, :, -1], field_map[:, :, 0])
+    row = jnp.where(row_half == 0, field_map[:, -1], field_map[:, 0])
+    point = jnp.where(col_half == 0, row[:, -1], row[:, 0])
+    column = column.reshape(items, side // 2, 2, channels).transpose(0, 2, 1, 3)
+    return send_rims(column, row, point)
+
+
+def woven_rims(woven, row_half, col_half):
+    column = jnp.where(col_half == 0, woven[:, -1], woven[:, 0])
+    row = jnp.where(row_half == 0, woven[:, :, -1], woven[:, :, 0])
+    point = jnp.where(col_half == 0, row[:, -1], row[:, 0])
+    return send_rims(column, row, point)
+
+
+def weave(side):
+    area = side * side
+    place = lax.broadcasted_iota(jnp.int32, (area, area), 0)
+    token = lax.broadcasted_iota(jnp.int32, (area, area), 1)
+    column = place // side
+    parity = (place % side) // (side // 2)
+    source = (2 * (place % (side // 2)) + parity) * side + column
+    return jnp.where(token == source, 1.0, 0.0).astype(jnp.bfloat16)
+
+
+def weave_rows(target, source, items, side):
+    area = side * side
+    order = weave(side)
+    for item in range(items):
+        span = slice(item * area, (item + 1) * area)
+        target[span, :] = jnp.dot(
+            order, source[span, :], preferred_element_type=jnp.float32
+        ).astype(jnp.bfloat16)
+
+
+def unweave_rows(target, source, items, side):
+    area = side * side
+    order = weave(side)
+    across = (((0,), (0,)), ((), ()))
+    for item in range(items):
+        span = slice(item * area, (item + 1) * area)
+        exact = source[span, :]
+        high = exact.astype(jnp.bfloat16)
+        low = (exact - high.astype(jnp.float32)).astype(jnp.bfloat16)
+        target[span, :] = lax.dot_general(
+            order, high, across, preferred_element_type=jnp.float32
+        ) + lax.dot_general(order, low, across, preferred_element_type=jnp.float32)
+
+
+def fill_padded(padded, tile_of, column, row, point, upper, left, items, side):
     high = side + 2
-    area = side * side
-    count = 4 * side + 8
+    width = padded.shape[-1]
+    right = 1.0 - left
+    lower = 1.0 - upper
+    where = lax.broadcasted_iota(jnp.int32, (SUBLANES, width), 0)
+
+    def put(spot, tile, edge):
+        even = tile[:SUBLANES]
+        odd = tile[SUBLANES:]
+        padded[spot, 0] = jnp.where(where == 0, edge * upper, pltpu.roll(odd, 1, 0))
+        padded[spot, 1] = even
+        padded[spot, 2] = odd
+        padded[spot, 3] = jnp.where(
+            where == SUBLANES - 1, edge * lower, pltpu.roll(even, SUBLANES - 1, 0)
+        )
+
     for item in range(items):
-        top = item * high
-        block = inner[item * area : (item + 1) * area]
-        padded[top + 1 : top + 1 + side, INSET : INSET + side, :] = block.reshape(side, side, -1)
-        base = item * count
-        padded[top, INSET : INSET + side, :] = rim[base + 2 * side : base + 3 * side, :]
-        padded[top + side + 1, INSET : INSET + side, :] = rim[base + 3 * side : base + 4 * side, :]
-        for corner, (row, col) in enumerate(
-            [(0, INSET - 1), (0, INSET + side), (side + 1, INSET - 1), (side + 1, INSET + side)]
-        ):
-            at = base + 4 * side + corner
-            padded[top + row, col : col + 1, :] = rim[at : at + 1, :]
-        for row in range(side):
-            padded[top + 1 + row, INSET - 1 : INSET, :] = rim[base + row : base + row + 1, :]
-            at = base + side + row
-            padded[top + 1 + row, INSET + side : INSET + side + 1, :] = rim[at : at + 1, :]
+        rim = column[item * side : (item + 1) * side]
+        corner = point[item : item + 1]
+        put(item * high, rim * left, corner * left)
+        put(item * high + high - 1, rim * right, corner * right)
+
+    def some_tiles(trip, carry):
+        base = trip * UNROLL
+        spot = base + 2 * (base // side) + 1
+        for more in range(UNROLL):
+            put(spot + more, tile_of(base + more), row[pl.ds(base + more, 1), :])
+        return carry
+
+    lax.fori_loop(0, items * side // UNROLL, some_tiles, 0)
+
+
+def column_windows(padded, at, lanes):
+    return [padded[at + tap % 3, tap // 3 : tap // 3 + 2, :, lanes] for tap in range(9)]
+
+
+def summed_windows(windows, weights):
+    parts = [windows[tap] * weights[tap] for tap in range(9)]
+    while len(parts) > 1:
+        joined = [parts[i] + parts[i + 1] for i in range(0, len(parts) - 1, 2)]
+        parts = joined + parts[len(parts) - len(parts) % 2 :]
+    return parts[0]
+
+
+def as_wide(values):
+    return values.astype(jnp.bfloat16).astype(jnp.float32)
 
 
 def ffn_kernel(
     items,
     side,
+    halves_ref,
     second_ref,
-    rim_ref,
+    column_ref,
+    row_ref,
+    point_ref,
     d_two_ref,
     w_up_ref,
     w_down_ref,
@@ -236,130 +296,189 @@
     down_ref,
     tap_grad_ref,
     padded,
-    rim,
+    row,
     act,
     d_act,
+    second,
+    d_two,
+    total,
 ):
+    step = pl.program_id(0)
     chunk = w_up_ref.shape[1]
     low = jnp.bfloat16
-    raised = jnp.dot(second_ref[...], w_up_ref[...], preferred_element_type=jnp.float32)
-    rim[...] = (
-        jnp.dot(rim_ref[...], w_up_ref[...], preferred_element_type=jnp.float32)
-        .astype(low)
-        .astype(jnp.float32)
-    )
-    fill_padded(padded, raised.astype(low).astype(jnp.float32), rim, items, side)
+
+    @pl.when(step == 0)
+    def _():
+        weave_rows(second, second_ref, items, side)
+        weave_rows(d_two, d_two_ref, items, side)
+
+    def raise_up(rows):
+        return as_wide(jnp.dot(rows, w_up_ref[...], preferred_element_type=jnp.float32))
+
+    def tile_of(number):
+        return d_act[pl.ds(pl.multiple_of(number * side, side), side), :]
+
+    d_act[...] = raise_up(second[...])
+    row[...] = raise_up(row_ref[...])
+    fill_padded(
+        padded,
+        tile_of,
+        raise_up(column_ref[...]),
+        row,
+        raise_up(point_ref[...]),
+        halves_ref[0],
+        halves_ref[1],
+        items,
+        side,
+    )
     d_act[...] = lax.dot_general(
-        d_two_ref[...], w_down_ref[...], (((1,), (1,)), ((), ())), preferred_element_type=jnp.float32
+        d_two[...], w_down_ref[...], (((1,), (1,)), ((), ())), preferred_element_type=jnp.float32
     )
     for lane in range(0, chunk, LANES):
         lanes = slice(lane, lane + LANES)
         weights = [taps_ref[tap : tap + 1, lanes] for tap in range(9)]
-        sums = tuple(jnp.zeros((8, LANES), jnp.float32) for _ in range(9))
-        for item in range(items):
-
-            def one_row(row, sums, item=item):
-                top = item * (side + 2) + row
-                at = pl.ds(pl.multiple_of(item * side * side + row * side, side), side)
-                windows = [
-                    padded[top + tap // 3, INSET - 1 + tap % 3 : INSET - 1 + tap % 3 + side, lanes]
-                    for tap in range(9)
-                ]
-                v = windows[0] * weights[0]
-                for tap in range(1, 9):
-                    v = v + windows[tap] * weights[tap]
+
+        def some_columns(trip, sums):
+            base = trip * UNROLL
+            corner = base + 2 * (base // side)
+            for more in range(UNROLL):
+                number = base + more
+                start = corner + more
+                at = pl.ds(pl.multiple_of(number * side, side), side)
+                windows = column_windows(padded, start, lanes)
+                v = summed_windows(windows, weights)
                 square = v * v
                 bend = jnp.tanh(GELU_SCALE * v * (1.0 + GELU_CUBE * square))
                 half = 0.5 + 0.5 * bend
-                act[at, lanes] = (v * half).astype(low)
+                act[at, lanes] = (v * half).reshape(side, LANES).astype(low)
                 slope = half + 0.5 * v * (1.0 - bend * bend) * (
                     GELU_SCALE + (3.0 * GELU_CUBE * GELU_SCALE) * square
                 )
-                rounded = (d_act[at, lanes] * slope).astype(low)
+                rounded = (d_act[at, lanes] * slope.reshape(side, LANES)).astype(low)
                 d_filtered_ref[at, lanes] = rounded
-                wide = rounded.astype(jnp.float32)
+                wide = rounded.astype(jnp.float32).reshape(2, SUBLANES, LANES)
                 added = []
                 for tap in range(9):
                     product = windows[tap] * wide
-                    total = sums[tap]
-                    for part in range(0, side, 8):
-                        total = total + product[part : part + 8]
-                    added.append(total)
-                return tuple(added)
-
-            sums = lax.fori_loop(0, side, one_row, sums)
+                    added.append(sums[tap] + (product[0] + product[1]))
+                sums = tuple(added)
+            return sums
+
+        sums = tuple(jnp.zeros((SUBLANES, LANES), jnp.float32) for _ in range(9))
+        sums = lax.fori_loop(0, items * side // UNROLL, some_columns, sums)
         for tap in range(9):
             tap_grad_ref[tap : tap + 1, lanes] = jnp.sum(sums[tap], 0, keepdims=True)
     tap_grad_ref[9:, :] = jnp.zeros((tap_grad_ref.shape[0] - 9, chunk), jnp.float32)
     down_ref[...] = lax.dot_general(
-        act[...], d_two_ref[...], (((0,), (0,)), ((), ())), preferred_element_type=jnp.float32
+        act[...], d_two[...], (((0,), (0,)), ((), ())), preferred_element_type=jnp.float32
     ).astype(low)
-    part_two = jnp.dot(act[...], w_down_ref[...], preferred_element_type=jnp.float32)
-
-    @pl.when(pl.program_id(0) == 0)
+    part = jnp.dot(act[...], w_down_ref[...], preferred_element_type=jnp.float32)
+
+    @pl.when(step == 0)
     def _():
-        two_ref[...] = part_two
-
-    @pl.when(pl.program_id(0) > 0)
+        total[...] = part
+
+    @pl.when(step > 0)
     def _():
-        two_ref[...] += part_two
+        total[...] += part
+
+    @pl.when(step == pl.num_programs(0) - 1)
+    def _():
+        unweave_rows(two_ref, total, items, side)
 
 
 def ffn_back_kernel(
     items,
     side,
+    halves_ref,
     d_filtered_ref,
-    rim_ref,
-    flipped_ref,
+    column_ref,
+    row_ref,
+    point_ref,
+    second_ref,
     w_up_ref,
     taps_ref,
     up_ref,
     d_second_ref,
     padded,
-    rim,
+    row,
     d_raised,
+    flipped,
+    total,
 ):
+    step = pl.program_id(0)
     chunk = w_up_ref.shape[1]
     low = jnp.bfloat16
-    rim[...] = rim_ref[...].astype(jnp.float32)
-    fill_padded(padded, d_filtered_ref[...].astype(jnp.float32), rim, items, side)
+    area = side * side
+
+    @pl.when(step == 0)
+    def _():
+        order = weave(side)
+        for item in range(items):
+            span = slice(item * area, (item + 1) * area)
+            flipped[:, span] = lax.dot_general(
+                second_ref[span, :], order, (((0,), (1,)), ((), ())), preferred_element_type=jnp.float32
+            ).astype(low)
+
+    def tile_of(number):
+        at = pl.ds(pl.multiple_of(number * side, side), side)
+        return d_filtered_ref[at, :].astype(jnp.float32)
+
+    row[...] = row_ref[...].astype(jnp.float32)
+    fill_padded(
+        padded,
+        tile_of,
+        column_ref[...].astype(jnp.float32),
+        row,
+        point_ref[...].astype(jnp.float32),
+        halves_ref[0],
+        halves_ref[1],
+        items,
+        side,
+    )
     for lane in range(0, chunk, LANES):
         lanes = slice(lane, lane + LANES)
         weights = [taps_ref[8 - tap : 9 - tap, lanes] for tap in range(9)]
-        for item in range(items):
-
-            def one_row(row, carry, item=item):
-                top = item * (side + 2) + row
-                at = pl.ds(pl.multiple_of(item * side * side + row * side, side), side)
-                v = None
-                for tap in range(9):
-                    first = INSET - 1 + tap % 3
-                    term = padded[top + tap // 3, first : first + side, lanes] * weights[tap]
-                    v = term if v is None else v + term
-                d_raised[at, lanes] = v.astype(low)
-                return carry
-
-            lax.fori_loop(0, side, one_row, 0)
-    up_ref[...] = jnp.dot(
-        flipped_ref[...], d_raised[...], preferred_element_type=jnp.float32
-    ).astype(low)
+
+        def some_columns(trip, carry):
+            base = trip * UNROLL
+            corner = base + 2 * (base // side)
+            for more in range(UNROLL):
+                number = base + more
+                start = corner + more
+                at = pl.ds(pl.multiple_of(number * side, side), side)
+                v = summed_windows(column_windows(padded, start, lanes), weights)
+                d_raised[at, lanes] = v.reshape(side, LANES).astype(low)
+            return carry
+
+        lax.fori_loop(0, items * side // UNROLL, some_columns, 0)
+    up_ref[...] = jnp.dot(flipped[...], d_raised[...], preferred_element_type=jnp.float32).astype(
+        low
+    )
     part = lax.dot_general(
         d_raised[...], w_up_ref[...], (((1,), (1,)), ((), ())), preferred_element_type=jnp.float32
     )
 
-    @pl.when(pl.program_id(0) == 0)
+    @pl.when(step == 0)
     def _():
-        d_second_ref[...] = part
-
-    @pl.when(pl.program_id(0) > 0)
+        total[...] = part
+
+    @pl.when(step > 0)
     def _():
-        d_second_ref[...] += part
-
-
-def ffn_pass(second, rim, d_two, w_up, w_down, taps, items, side, chunk=256):
+        total[...] += part
+
+    @pl.when(step == pl.num_programs(0) - 1)
+    def _():
+        unweave_rows(d_second_ref, total, items, side)
+
+
+def padded_shape(items, side, chunk):
+    return pltpu.VMEM((items * (side + 2), 4, SUBLANES, chunk), jnp.float32)
+
+
+def ffn_pass(halves, second, rims, d_two, w_up, w_down, taps, items, side, chunk=256):
     tokens, channels = second.shape
     wide = w_up.shape[1]
-    rims = rim.shape[0]
     fixed = lambda step: (0, 0)
     columns = lambda step: (0, step)
     rows = lambda step: (step, 0)
@@ -367,8 +486,11 @@
         functools.partial(ffn_kernel, items, side),
         grid=(wide // chunk,),
         in_specs=[
+            pl.BlockSpec(memory_space=pltpu.SMEM),
             pl.BlockSpec((tokens, channels), fixed),
-            pl.BlockSpec((rims, channels), fixed),
+            pl.BlockSpec(rims[0].shape, fixed),
+            pl.BlockSpec(rims[1].shape, fixed),
+            pl.BlockSpec(rims[2].shape, fixed),
             pl.BlockSpec((tokens, channels), fixed),
             pl.BlockSpec((channels, chunk), columns),
             pl.BlockSpec((chunk, channels), rows),
@@ -387,10 +509,13 @@
             jax.ShapeDtypeStruct((16, wide), jnp.float32),
         ],
         scratch_shapes=[
-            pltpu.VMEM((items * (side + 2), side + 2 * INSET, chunk), jnp.float32),
-            pltpu.VMEM((rims, chunk), jnp.float32),
+            padded_shape(items, side, chunk),
+            pltpu.VMEM((items * side, chunk), jnp.float32),
             pltpu.VMEM((tokens, chunk), jnp.bfloat16),
             pltpu.VMEM((tokens, chunk), jnp.float32),
+            pltpu.VMEM((tokens, channels), jnp.bfloat16),
+            pltpu.VMEM((tokens, channels), jnp.bfloat16),
+            pltpu.VMEM((tokens, channels), jnp.float32),
         ],
         cost_estimate=pl.CostEstimate(
             flops=8 * tokens * channels * wide,
@@ -398,22 +523,24 @@
             transcendentals=tokens * wide,
         ),
         name="ffn",
-    )(second, rim, d_two, w_up, w_down, taps)
-
-
-def ffn_back_pass(d_filtered, rim, flipped, w_up, taps, items, side, chunk=256):
+    )(halves, second, *rims, d_two, w_up, w_down, taps)
+
+
+def ffn_back_pass(halves, d_filtered, rims, second, w_up, taps, items, side, chunk=256):
     tokens, wide = d_filtered.shape
     channels = w_up.shape[0]
-    rims = rim.shape[0]
     fixed = lambda step: (0, 0)
     columns = lambda step: (0, step)
     return pl.pallas_call(
         functools.partial(ffn_back_kernel, items, side),
         grid=(wide // chunk,),
         in_specs=[
+            pl.BlockSpec(memory_space=pltpu.SMEM),
             pl.BlockSpec((tokens, chunk), columns),
-            pl.BlockSpec((rims, chunk), columns),
-            pl.BlockSpec((channels, tokens), fixed),
+            pl.BlockSpec((rims[0].shape[0], chunk), columns),
+            pl.BlockSpec((rims[1].shape[0], chunk), columns),
+            pl.BlockSpec((rims[2].shape[0], chunk), columns),
+            pl.BlockSpec((tokens, channels), fixed),
             pl.BlockSpec((channels, chunk), columns),
             pl.BlockSpec((16, chunk), columns),
         ],
@@ -426,9 +553,11 @@
             jax.ShapeDtypeStruct((tokens, channels), jnp.float32),
         ],
         scratch_shapes=[
-            pltpu.VMEM((items * (side + 2), side + 2 * INSET, chunk), jnp.float32),
-            pltpu.VMEM((rims, chunk), jnp.float32),
+            padded_shape(items, side, chunk),
+            pltpu.VMEM((items * side, chunk), jnp.float32),
             pltpu.VMEM((tokens, chunk), jnp.bfloat16),
+            pltpu.VMEM((channels, tokens), jnp.bfloat16),
+            pltpu.VMEM((tokens, channels), jnp.float32),
         ],
         cost_estimate=pl.CostEstimate(
             flops=4 * tokens * channels * wide,
@@ -436,7 +565,7 @@
             transcendentals=0,
         ),
         name="ffn_back",
-    )(d_filtered, rim, flipped, w_up, taps)
+    )(halves, d_filtered, *rims, second, w_up, taps)
 
 
 def shards(
@@ -485,9 +614,11 @@
     d_branch_two = (grad_res * gate_f).astype(jnp.bfloat16)
     taps_ffn = jnp.pad(conv_ffn.astype(jnp.float32).T, ((0, 7), (0, 0)))
     flat_second = second.reshape(token_count, channels)
+    halves = jnp.stack([row_half, col_half]).astype(jnp.float32)
     branch_two, d_filtered, down_grad, tap_grad = ffn_pass(
+        halves,
         flat_second,
-        rim_exchange(second, row_half, col_half).reshape(-1, channels),
+        map_rims(second, row_half, col_half),
         d_branch_two.reshape(token_count, channels),
         w_up,
         w_down,
@@ -501,9 +632,10 @@
     d_gate_f = jnp.sum(grad_res * branch_two, (1, 2))
     d_filtered_map = d_filtered.reshape(item_count, half_side, half_side, -1)
     up_grad, d_second = ffn_back_pass(
+        halves,
         d_filtered,
-        rim_exchange(d_filtered_map, row_half, col_half).reshape(-1, w_up.shape[1]),
-        flat_second.T,
+        woven_rims(d_filtered_map, row_half, col_half),
+        flat_second,
         w_up,
         taps_ffn,
         item_count,

time: 638 us -> 629 us (0.986)
  other arithmetic: 120 us -> 160 us
  Pallas kernels: 126 us -> 96.2 us
  matrix products: 72.6 us -> 64.7 us
    concatenate x2 -> x0, local copies, waits for them, and re-layouts: 20 us -> none  [rim_exchange(): jnp.concatenate([kept(column, left), kept(column, ~left), kept(row, upper...]
    pallas_call x1, Pallas kernels: 83.1 us -> 66 us  [ffn_pass(): pl.pallas_call(functools.partial(ffn_kernel, items, side), grid=(wide //...]
    pallas_call x1, Pallas kernels: 42.5 us -> 30.3 us  [ffn_back_pass(): pl.pallas_call(functools.partial(ffn_back_kernel, items, side), grid=(wid...]
    reduce_sum x1 -> x2, other arithmetic: 0.5 us -> 12.7 us  [normed(): return centred * lax.rsqrt(variance + epsilon)]
    select_n x12 -> x6, other arithmetic: 16.7 us -> 4.78 us  [the longest x1 1.8 us: woven_rims(): column = jnp.where(col_half == 0, woven[:, -1], woven[:, 0])]
    reduce_sum x2 -> x3, other arithmetic: 3.75 us -> 14.7 us  [modulate(): return normed(field_map) * (1.0 + scale) + shift]
    reduce_sum x1, other arithmetic: 2.87 us -> 13.2 us  [shards(): d_gate_a = jnp.sum(d_hidden * branch, (1, 2))]
    reduce_sum x0 -> x6, local copies, waits for them, and re-layouts: none -> 10.1 us  [the longest x2 3.36 us: normed(): centred = field_map - average]
  transfers between devices with their start and end apart: 42 -> 42, of which waited for: 19 -> 20; matrix products, arithmetic and copies ran while one was open for 46% -> 49% of each run, Pallas kernels for 7% -> 5%
where the time goes in v3:
time: 629 us; the launch traced here: 619 us
  local copies, waits for them, and re-layouts  163 us (26%)
  other arithmetic  160 us (25%)
  Pallas kernels  96.2 us (15%)
  waiting for transfers between devices  75 us (12%)
  matrix products  64.7 us (10%)
  starting transfers between devices  58 us (9%)
    pallas_call x1, Pallas kernels, ffn_pass(): pl.pallas_call(functools.partial(ffn_kernel, items, side), grid=(wide //...  66 us
    ppermute x32, waiting for transfers between devices, from_partner(): lax.ppermute(shard, axis, [(i, i ^ 1 << bit) for i in range(lax.axis_size...  53.3 us
    ppermute x32, starting transfers between devices, from_partner(): lax.ppermute(shard, axis, [(i, i ^ 1 << bit) for i in range(lax.axis_size...  35.5 us
    pallas_call x1, Pallas kernels, ffn_back_pass(): pl.pallas_call(functools.partial(ffn_back_kernel, items, side), grid=(wid...  30.3 us
    unnamed x189, local copies, waits for them, and re-layouts  21 us
    convert_element_type x16, other arithmetic, halving_sum(): held = held.astype(jnp.bfloat16)  15.1 us
    reduce_sum x3, other arithmetic, modulate(): return normed(field_map) * (1.0 + scale) + shift  14.7 us
    all_to_all x2, waiting for transfers between devices, to_groups(): lax.all_to_all(pieces, 'narrow', split_axis=1, concat_axis=1, tiled=True)  13.6 us
  transfers between devices with their start and end apart: 42, of which 20 were waited for; matrix products, arithmetic and copies ran while one was open for 49% of the time, Pallas kernels for 5%

profile of v3, /device:TPU:0, one launch (start us, length us, event | category | flops | bytes accessed | tf_op | source)
XLA Modules:
  0.0 619.5 jit_solution(8007642704057203171)
XLA Ops:
  34.2 5.1 maximum_maximum_fusion
  39.4 6.1 fusion.45
  46.8 4.7 all-to-all-start
  59.1 8.3 %all-to-all-done = bf16[3,4,64,768]{3,2,0,1:T(8,128)(2,1)} async-done(((bf16[3,4,64,768]{3,2,0,1:T(8,128)(2,1)}), bf16[3,4,64,768]{3,2,0,1:T(8,128)(2,1)}, u32[]{:S(2)}, u32[]{:S(2)}) %all-to-all-start) | async-done | bytes 1179680 | tf_op jit(solution)/shard_map/all_to_all | solution.py:90
  74.2 5.8 copy.315
  87.4 4.6 fusion.58
  92.0 4.6 reshape_reshape.12
  96.6 5.1 copy.320
  159.7 66.0 %ffn.1 = (f32[768,768]{1,0:T(8,128)}, bf16[768,3072]{1,0:T(8,128)(2,1)}, bf16[3072,768]{1,0:T(8,128)(2,1)}, f32[16,3072]{1,0:T(8,128)}) custom-call(f32[2]{0:T(128)} %add_convert_fusion.4.halves_ref, bf16[768,768]{1,0:T(8,128)(2,1)} %bitcast.340, bf16[48,768]{1,0:T(8,128)(2,1)} %bitcast.350, bf16[48,768]{1,0:T(8,128)(2,1)} %bitcast.351, ...), custom_call_target="tpu_custom_call" | custom-call | flops 14495514624 | bytes 37748736 | tf_op jit(solution)/shard_map/ffn/pallas_call | solution.py:485
  248.1 30.3 %ffn_back.1 = (bf16[768,3072]{1,0:T(8,128)(2,1)}, f32[768,768]{1,0:T(8,128)}) custom-call(f32[2]{0:T(128)} %add_convert_fusion.4.halves_ref, bf16[768,3072]{1,0:T(8,128)(2,1)} %get-tuple-element.17.d_filtered_ref, bf16[48,3072]{1,0:T(8,128)(2,1)} %bitcast.49.column_ref, bf16[48,3072]{1,0:T(8,128)(2,1)} %bitcast.346, bf16[8,3072]{1,0:T(8,128)(2,1)} %pad.22.point_ref, ...), custom_call_target="tpu_custom_call" | custom-call | flops 7247757312 | bytes 18874368 | tf_op jit(solution)/shard_map/ffn_back/pallas_call | solution.py:534
  293.1 7.1 %fusion.20 = (f32[3,768]{1,0:T(4,128)}, f32[3,16,16]{0,2,1:T(8,128)}) fusion(f32[3,16,16,768]{3,2,1,0:T(8,128)} %bitcast.305, f32[3,16,16,768]{3,0,2,1:T(4,128)} %get-tuple-element.114, f32[3,16,16]{0,2,1:T(8,128)} %copy.328, f32[3,16,16]{0,2,1:T(8,128)} %copy.326, f32[3,16,16]{0,2,1:T(8,128)} %copy.342, f32[3,768]{1,0:T(4,128)S(1)} %copy-done.50), kind=kLoop, calls=%fused_computation.59 | loop fusion | flops 5895168 | bytes 4749312 | tf_op jit(solution)/shard_map/transpose(jvp())/reduce_sum | solution.py:30
  304.8 13.2 %fusion.15 = (f32[3,768]{1,0:T(4,128)}, f32[3,16,16,768]{3,0,2,1:T(4,128)S(1)}, f32[3,768]{1,0:T(4,128)}, bf16[3,16,16,768]{3,0,2,1:T(4,128)(2,1)}) fusion(f32[3,16,16,768]{3,2,1,0:T(8,128)} %copy-done.17, f32[3,16,16]{0,2,1:T(8,128)} %copy.344, f32[3,16,16]{0,2,1:T(8,128)} %copy.342, f32[3,16,16,768]{3,0,2,1:T(4,128)} %get-tuple-element.114, ...), kind=kLoop, calls=%fused_computation.54 | loop fusion | flops 10022400 | bytes 15384588 | tf_op jit(solution)/shard_map/reduce_sum | solution.py:647
  344.7 5.3 all-to-all-done.2
  350.0 5.1 copy.348
  355.1 4.5 reshape_reshape.13
  359.6 10.9 %multiply_reduce_fusion = (f32[3,12,256]{2,1,0:T(8,128)}, f32[3,12,256,256]{2,3,1,0:T(8,128)}) fusion(f32[3,12,256,256]{2,3,1,0:T(8,128)} %copy-done.1, f32[3,12,256]{2,1,0:T(8,128)} %log_add_fusion, bf16[3,256,12,64]{1,3,2,0:T(8,128)(2,1)} %reshape_reshape.13, bf16[3,256,3,12,64]{1,4,3,2,0:T(8,128)(2,1)} %bitcast.311), kind=kOutput, calls=%fused_computation.10 | convolution fusion | flops 311417856 | bytes 21319680 | tf_op jit(solution)/shard_map/iqhe,ikhe->ihqk/dot_general | solution.py:658
  370.5 11.3 %multiply_convert_fusion = bf16[3,12,256,256]{2,3,1,0:T(8,128)(2,1)} fusion(f32[3,12,256,256]{2,3,1,0:T(8,128)} %get-tuple-element.162, f32[3,12,256,256]{2,3,1,0:T(8,128)} %copy-done.1, f32[3,12,256]{2,1,0:T(8,128)} %get-tuple-element.161, f32[3,12,256]{2,1,0:T(8,128)} %log_add_fusion), kind=kLoop, calls=%fused_computation.9 | loop fusion | flops 11796480 | bytes 23666688 | tf_op jit(solution)/shard_map/convert_element_type | solution.py:662
  388.8 5.5 fusion.51
  399.3 4.7 all-to-all-start.3
  404.0 5.3 bitcast_convert_fusion
  412.9 7.0 %all-to-all-done.3 = bf16[3,4,64,768]{3,2,0,1:T(8,128)(2,1)} async-done(((bf16[3,4,64,768]{3,2,0,1:T(8,128)(2,1)}), bf16[3,4,64,768]{3,2,0,1:T(8,128)(2,1)}, u32[]{:S(2)}, u32[]{:S(2)}) %all-to-all-start.3) | async-done | bytes 1179680 | tf_op jit(solution)/shard_map/all_to_all | solution.py:97
  422.3 9.5 %fusion.44 = (bf16[768]{0:T(1024)(128)(2,1)S(1)}, bf16[768]{0:T(1024)(128)(2,1)S(1)}, bf16[768]{0:T(1024)(128)(2,1)S(1)}, bf16[768]{0:T(1024)(128)(2,1)S(1)}, bf...) fusion(bf16[3,16,16,768]{3,0,2,1:T(4,128)(2,1)S(1)} %bitcast.30, ...), kind=kLoop, calls=%fused_computation.83 | loop fusion | flops 18278400 | bytes 9596928 | tf_op jit(solution)/shard_map/reduce_sum | solution.py:81
  463.0 5.0 pad_maximum_fusion.2
  468.0 9.6 %fusion.21 = (f32[3,16,16]{0,2,1:T(8,128)}, bf16[3,16,16,768]{3,0,2,1:T(4,128)(2,1)}) fusion(f32[3,16,16,768]{3,0,2,1:T(4,128)S(1)} %bitcast.297, f32[3,768]{1,0:T(4,128)S(1)} %copy-done.49, f32[3,16,16]{0,2,1:T(8,128)S(1)} %bitcast.333, f32[768]{0:T(1024)S(1)} %copy-done.71, bf16[3,17,18,768]{3,0,2,1:T(4,128)(2,1)S(1)} %get-tuple-element.126, ...), kind=kLoop, calls=%fused_computation.60 | loop fusion | flops 20053248 | bytes 11986944 | tf_op jit(solution)/shard_map/transpose(jvp())/reduce_sum | solution.py:26
  482.2 5.8 fusion.30
  498.3 4.8 add_convert_fusion
  505.9 4.9 fusion.89
  532.2 7.7 %collective-permute-done.17 = f32[4,3,4608]{2,1,0:T(4,128)S(1)} collective-permute-done((f32[4,3,4608]{2,1,0:T(4,128)S(1)}, f32[4,3,4608]{2,1,0:T(4,128)S(1)}, u32[]{:S(2)}, u32[]{:S(2)}) %collective-permute-start.17) | collective-permute-done | bytes 221216 | tf_op jit(solution)/shard_map/ppermute | solution.py:19
  549.1 6.5 %collective-permute-done.20 = bf16[2,2,24,1536]{3,2,1,0:T(8,128)(2,1)S(1)} collective-permute-done((bf16[2,2,24,1536]{3,2,1,0:T(8,128)(2,1)S(1)}, bf16[2,2,24,1536]{3,2,1,0:T(8,128)(2,1)S(1)}, u32[]{:S(2)}, u32[]{:S(2)}) %collective-permute-start.20) | collective-permute-done | bytes 294944 | tf_op jit(solution)/shard_map/ppermute | solution.py:19
  574.4 5.6 collective-permute-done.24
  594.3 4.6 collective-permute-done.26
  613.6 5.0 collective-permute-done.32
  (450 shorter events, 327.3 us)
Async XLA Ops:
  27.8 6.3 %collective-permute-start.1 = (bf16[3,1,18,768]{3,0,2,1:T(4,128)(2,1)S(1)}, bf16[3,1,18,768]{3,0,2,1:T(4,128)(2,1)S(1)}, u32[]{:S(2)}, u32[]{:S(2)}) collective-permute-start(bf16[3,1,18,768]{3,0,2,1:T(4,128)(2,1)S(1)} %fusion.83), channel_id=1, source_target_pairs={{0,2},{1,3},{2,0},{3,1},{4,6},{5,7},{6,4},{7,5},{8,10},{9,11},{10,... | collective-permute-start | bytes 248840 | tf_op jit(solution)/shard_map/ppermute | solution.py:19
  46.8 20.6 %all-to-all-start = ((bf16[3,4,64,768]{3,2,0,1:T(8,128)(2,1)}), bf16[3,4,64,768]{3,2,0,1:T(8,128)(2,1)}, u32[]{:S(2)}, u32[]{:S(2)}) async-start(bf16[3,4,64,768]{3,2,0,1:T(8,128)(2,1)} %bitcast.325), calls=%async_computation | async-start | bytes 2359296 | tf_op jit(solution)/shard_map/all_to_all | solution.py:90
  57.5 48.6 %collective-permute-start.13 = (bf16[2,3,768]{2,1,0:T(4,128)(2,1)}, bf16[2,3,768]{2,1,0:T(4,128)(2,1)}, u32[]{:S(2)}, u32[]{:S(2)}) collective-permute-start(bf16[2,3,768]{2,1,0:T(4,128)(2,1)} %pad_maximum_fusion.17), channel_id=1, source_target_pairs={{0,8},{4,12},{8,0},{12,4},{16,24},{20,28},{24,16},{28,20},{1,9},{5... | collective-permute-start | bytes 27656 | tf_op jit(solution)/shard_map/ppermute | solution.py:19
  101.7 20.8 %all-to-all-start.1 = ((bf16[3,4,64,768]{3,2,0,1:T(8,128)(2,1)}), bf16[3,4,64,768]{3,2,0,1:T(8,128)(2,1)}, u32[]{:S(2)}, u32[]{:S(2)}) async-start(bf16[3,4,64,768]{3,2,0,1:T(8,128)(2,1)} %copy.320), calls=%async_computation.1 | async-start | bytes 2359296 | tf_op jit(solution)/shard_map/all_to_all | solution.py:97
  108.2 11.4 %collective-permute-start.14 = (bf16[4,3,768]{2,1,0:T(4,128)(2,1)}, bf16[4,3,768]{2,1,0:T(4,128)(2,1)}, u32[]{:S(2)}, u32[]{:S(2)}) collective-permute-start(bf16[4,3,768]{2,1,0:T(4,128)(2,1)} %pad_maximum_fusion.16), channel_id=1, source_target_pairs={{0,16},{4,20},{8,24},{12,28},{16,0},{20,4},{24,8},{28,12},{1,17},{... | collective-permute-start | bytes 55304 | tf_op jit(solution)/shard_map/ppermute | solution.py:19
  152.5 6.5 %collective-permute-start.3 = (bf16[3,16,768]{2,0,1:T(4,128)(2,1)S(1)}, bf16[3,16,768]{2,0,1:T(4,128)(2,1)S(1)}, u32[]{:S(2)}, u32[]{:S(2)}) collective-permute-start(bf16[3,16,768]{2,0,1:T(4,128)(2,1)S(1)} %fusion.88), channel_id=1, source_target_pairs={{0,2},{1,3},{2,0},{3,1},{4,6},{5,7},{6,4},{7,5},{8,10},{9,11},{10,... | collective-permute-start | bytes 221192 | tf_op jit(solution)/shard_map/ppermute | solution.py:176
  230.6 15.6 %collective-permute-start.6 = (bf16[3,16,3072]{2,0,1:T(4,128)(2,1)}, bf16[3,16,3072]{2,0,1:T(4,128)(2,1)}, u32[]{:S(2)}, u32[]{:S(2)}) collective-permute-start(bf16[3,16,3072]{2,0,1:T(4,128)(2,1)} %fusion.76), channel_id=1, source_target_pairs={{0,2},{1,3},{2,0},{3,1},{4,6},{5,7},{6,4},{7,5},{8,10},{9,11},{10,... | collective-permute-start | bytes 884744 | tf_op jit(solution)/shard_map/ppermute | solution.py:176
  238.1 278.6 %collective-permute-start.33 = (bf16[2,2,2,2,96,768]{5,4,0,1,2,3:T(8,128)(2,1)}, bf16[2,2,2,2,96,768]{5,4,0,1,2,3:T(8,128)(2,1)}, u32[]{:S(2)}, u32[]{:S(2)}) collective-permute-start(bf16[2,2,2,2,96,768]{5,4,0,1,2,3:T(8,128)(2,1)} %bitcast.289), channel_id=1, source_target_pairs={{0,1},{1,0},{2,3},{3,2},{4,5},{5,4},{6,7},{7,6},{8,9},{9,8},{10,11... | collective-permute-start | bytes 7077896 | tf_op jit(solution)/shard_map/ppermute | solution.py:19
  238.5 6.4 %collective-permute-start.7 = (bf16[3,3072]{1,0:T(4,128)(2,1)}, bf16[3,3072]{1,0:T(4,128)(2,1)}, u32[]{:S(2)}, u32[]{:S(2)}) collective-permute-start(bf16[3,3072]{1,0:T(4,128)(2,1)} %fusion.90), channel_id=1, source_target_pairs={{0,3},{1,2},{2,1},{3,0},{4,7},{5,6},{6,5},{7,4},{8,11},{9,10},{10,... | collective-permute-start | bytes 55304 | tf_op jit(solution)/shard_map/ppermute | solution.py:177
  239.4 8.7 %collective-permute-start.5 = (bf16[3,16,3072]{2,1,0:T(8,128)(2,1)}, bf16[3,16,3072]{2,1,0:T(8,128)(2,1)}, u32[]{:S(2)}, u32[]{:S(2)}) collective-permute-start(bf16[3,16,3072]{2,1,0:T(8,128)(2,1)} %fusion.78), channel_id=1, source_target_pairs={{0,1},{1,0},{2,3},{3,2},{4,5},{5,4},{6,7},{7,6},{8,9},{9,8},{10,11... | collective-permute-start | bytes 884744 | tf_op jit(solution)/shard_map/ppermute | solution.py:175
  284.2 242.1 %collective-permute-start.28 = (bf16[2,2,2,2,24,3072]{5,4,0,1,3,2:T(8,128)(2,1)}, bf16[2,2,2,2,24,3072]{5,4,0,1,3,2:T(8,128)(2,1)}, u32[]{:S(2)}, u32[]{:S(2)}) collective-permute-start(bf16[2,2,2,2,24,3072]{5,4,0,1,3,2:T(8,128)(2,1)} %bitcast.290), channel_id=1, source_target_pairs={{0,1},{1,0},{2,3},{3,2},{4,5},{5,4},{6,7},{7,6},{8,9},{9,8},{10,11... | collective-permute-start | bytes 7077896 | tf_op jit(solution)/shard_map/ppermute | solution.py:19
  329.6 20.3 %all-to-all-start.2 = ((bf16[3,4,64,768]{3,2,0,1:T(8,128)(2,1)}), bf16[3,4,64,768]{3,2,0,1:T(8,128)(2,1)}, u32[]{:S(2)}, u32[]{:S(2)}) async-start(bf16[3,4,64,768]{3,2,0,1:T(8,128)(2,1)} %bitcast.324), calls=%async_computation.2 | async-start | bytes 2359296 | tf_op jit(solution)/shard_map/all_to_all | solution.py:90
  399.3 20.6 %all-to-all-start.3 = ((bf16[3,4,64,768]{3,2,0,1:T(8,128)(2,1)}), bf16[3,4,64,768]{3,2,0,1:T(8,128)(2,1)}, u32[]{:S(2)}, u32[]{:S(2)}) async-start(bf16[3,4,64,768]{3,2,0,1:T(8,128)(2,1)} %copy.354), calls=%async_computation.3 | async-start | bytes 2359296 | tf_op jit(solution)/shard_map/all_to_all | solution.py:97
  412.4 101.0 %collective-permute-start.18 = (bf16[2,2,2,2,24,1536]{5,4,3,2,1,0:T(8,128)(2,1)}, bf16[2,2,2,2,24,1536]{5,4,3,2,1,0:T(8,128)(2,1)}, u32[]{:S(2)}, u32[]{:S(2)}) collective-permute-start(bf16[2,2,2,2,24,1536]{5,4,3,2,1,0:T(8,128)(2,1)} %dynamic-slice_bitcast_fusion.2), channel_id=1, source_target_pairs={{0,1},{1,0},{2,3},{3,2},{4,5},{5,4},{6,7},{7,6},{8,9},{9,8},{10,11... | collective-permute-start | bytes 3538952 | tf_op jit(solution)/shard_map/ppermute | solution.py:19
  460.2 96.1 %collective-permute-start.23 = (bf16[2,2,2,2,24,1664]{5,4,0,1,2,3:T(8,128)(2,1)}, bf16[2,2,2,2,24,1664]{5,4,0,1,2,3:T(8,128)(2,1)}, u32[]{:S(2)}, u32[]{:S(2)}) collective-permute-start(bf16[2,2,2,2,24,1664]{5,4,0,1,2,3:T(8,128)(2,1)} %bitcast.291), channel_id=1, source_target_pairs={{0,1},{1,0},{2,3},{3,2},{4,5},{5,4},{6,7},{7,6},{8,9},{9,8},{10,11... | collective-permute-start | bytes 3833864 | tf_op jit(solution)/shard_map/ppermute | solution.py:19
  497.8 6.4 %collective-permute-start.11 = (f32[3,4608]{1,0:T(4,128)S(1)}, f32[3,4608]{1,0:T(4,128)S(1)}, u32[]{:S(2)}, u32[]{:S(2)}) collective-permute-start(f32[3,4608]{1,0:T(4,128)S(1)} %add.358), channel_id=1, source_target_pairs={{0,2},{1,3},{2,0},{3,1},{4,6},{5,7},{6,4},{7,5},{8,10},{9,11},{10,... | collective-permute-start | bytes 165896 | tf_op jit(solution)/shard_map/ppermute | solution.py:19
  504.3 14.7 %collective-permute-start.15 = (f32[1,3,4608]{2,1,0:T(4,128)S(1)}, f32[1,3,4608]{2,1,0:T(4,128)S(1)}, u32[]{:S(2)}, u32[]{:S(2)}) collective-permute-start(f32[1,3,4608]{2,1,0:T(4,128)S(1)} %bitcast.335), channel_id=1, source_target_pairs={{0,4},{4,0},{8,12},{12,8},{16,20},{20,16},{24,28},{28,24},{1,5},{5... | collective-permute-start | bytes 165896 | tf_op jit(solution)/shard_map/ppermute | solution.py:19
  516.1 26.9 %collective-permute-start.19 = (bf16[2,2,2,24,1536]{4,3,2,1,0:T(8,128)(2,1)}, bf16[2,2,2,24,1536]{4,3,2,1,0:T(8,128)(2,1)}, u32[]{:S(2)}, u32[]{:S(2)}) collective-permute-start(bf16[2,2,2,24,1536]{4,3,2,1,0:T(8,128)(2,1)} %dynamic-slice_bitcast_fusion.6), channel_id=1, source_target_pairs={{0,4},{4,0},{8,12},{12,8},{16,20},{20,16},{24,28},{28,24},{1,5},{5... | collective-permute-start | bytes 1769480 | tf_op jit(solution)/shard_map/ppermute | solution.py:19
  521.8 45.9 %collective-permute-start.34 = (bf16[2,2,2,96,768]{4,3,0,1,2:T(8,128)(2,1)}, bf16[2,2,2,96,768]{4,3,0,1,2:T(8,128)(2,1)}, u32[]{:S(2)}, u32[]{:S(2)}) collective-permute-start(bf16[2,2,2,96,768]{4,3,0,1,2:T(8,128)(2,1)} %dynamic-slice_bitcast_fusion), channel_id=1, source_target_pairs={{0,2},{1,3},{2,0},{3,1},{4,6},{5,7},{6,4},{7,5},{8,10},{9,11},{10,... | collective-permute-start | bytes 3538952 | tf_op jit(solution)/shard_map/ppermute | solution.py:19
  524.7 15.1 %collective-permute-start.17 = (f32[4,3,4608]{2,1,0:T(4,128)S(1)}, f32[4,3,4608]{2,1,0:T(4,128)S(1)}, u32[]{:S(2)}, u32[]{:S(2)}) collective-permute-start(f32[4,3,4608]{2,1,0:T(4,128)S(1)} %pad_maximum_fusion.8), channel_id=1, source_target_pairs={{0,16},{4,20},{8,24},{12,28},{16,0},{20,4},{24,8},{28,12},{1,17},{... | collective-permute-start | bytes 663560 | tf_op jit(solution)/shard_map/ppermute | solution.py:19
  530.7 40.2 %collective-permute-start.29 = (bf16[2,2,2,24,3072]{4,3,0,1,2:T(8,128)(2,1)}, bf16[2,2,2,24,3072]{4,3,0,1,2:T(8,128)(2,1)}, u32[]{:S(2)}, u32[]{:S(2)}) collective-permute-start(bf16[2,2,2,24,3072]{4,3,0,1,2:T(8,128)(2,1)} %dynamic-slice_bitcast_fusion.1), channel_id=1, source_target_pairs={{0,4},{4,0},{8,12},{12,8},{16,20},{20,16},{24,28},{28,24},{1,5},{5... | collective-permute-start | bytes 3538952 | tf_op jit(solution)/shard_map/ppermute | solution.py:19
  544.6 11.1 %collective-permute-start.20 = (bf16[2,2,24,1536]{3,2,1,0:T(8,128)(2,1)S(1)}, bf16[2,2,24,1536]{3,2,1,0:T(8,128)(2,1)S(1)}, u32[]{:S(2)}, u32[]{:S(2)}) collective-permute-start(bf16[2,2,24,1536]{3,2,1,0:T(8,128)(2,1)S(1)} %dynamic-slice_bitcast_fusion.10), channel_id=1, source_target_pairs={{0,2},{1,3},{2,0},{3,1},{4,6},{5,7},{6,4},{7,5},{8,10},{9,11},{10,... | collective-permute-start | bytes 884744 | tf_op jit(solution)/shard_map/ppermute | solution.py:19
  562.6 17.3 %collective-permute-start.24 = (bf16[2,2,2,24,1664]{4,3,0,1,2:T(8,128)(2,1)S(1)}, bf16[2,2,2,24,1664]{4,3,0,1,2:T(8,128)(2,1)S(1)}, u32[]{:S(2)}, u32[]{:S(2)}) collective-permute-start(bf16[2,2,2,24,1664]{4,3,0,1,2:T(8,128)(2,1)S(1)} %dynamic-slice_bitcast_fusion.3), channel_id=1, source_target_pairs={{0,2},{1,3},{2,0},{3,1},{4,6},{5,7},{6,4},{7,5},{8,10},{9,11},{10,... | collective-permute-start | bytes 1916936 | tf_op jit(solution)/shard_map/ppermute | solution.py:19
  569.4 15.2 %collective-permute-start.35 = (bf16[2,2,96,768]{3,2,0,1:T(8,128)(2,1)S(1)}, bf16[2,2,96,768]{3,2,0,1:T(8,128)(2,1)S(1)}, u32[]{:S(2)}, u32[]{:S(2)}) collective-permute-start(bf16[2,2,96,768]{3,2,0,1:T(8,128)(2,1)S(1)} %dynamic-slice_bitcast_fusion.4), channel_id=1, source_target_pairs={{0,4},{4,0},{8,12},{12,8},{16,20},{20,16},{24,28},{28,24},{1,5},{5... | collective-permute-start | bytes 1769480 | tf_op jit(solution)/shard_map/ppermute | solution.py:19
  572.7 16.2 %collective-permute-start.30 = (bf16[2,2,24,3072]{3,2,0,1:T(8,128)(2,1)S(1)}, bf16[2,2,24,3072]{3,2,0,1:T(8,128)(2,1)S(1)}, u32[]{:S(2)}, u32[]{:S(2)}) collective-permute-start(bf16[2,2,24,3072]{3,2,0,1:T(8,128)(2,1)S(1)} %dynamic-slice_bitcast_fusion.5), channel_id=1, source_target_pairs={{0,2},{1,3},{2,0},{3,1},{4,6},{5,7},{6,4},{7,5},{8,10},{9,11},{10,... | collective-permute-start | bytes 1769480 | tf_op jit(solution)/shard_map/ppermute | solution.py:19
  580.2 7.8 %collective-permute-start.25 = (bf16[2,2,24,1664]{3,2,0,1:T(8,128)(2,1)S(1)}, bf16[2,2,24,1664]{3,2,0,1:T(8,128)(2,1)S(1)}, u32[]{:S(2)}, u32[]{:S(2)}) collective-permute-start(bf16[2,2,24,1664]{3,2,0,1:T(8,128)(2,1)S(1)} %dynamic-slice_bitcast_fusion.7), channel_id=1, source_target_pairs={{0,4},{4,0},{8,12},{12,8},{16,20},{20,16},{24,28},{28,24},{1,5},{5... | collective-permute-start | bytes 958472 | tf_op jit(solution)/shard_map/ppermute | solution.py:19
  584.7 9.4 %collective-permute-start.36 = (bf16[2,96,768]{2,1,0:T(8,128)(2,1)S(1)}, bf16[2,96,768]{2,1,0:T(8,128)(2,1)S(1)}, u32[]{:S(2)}, u32[]{:S(2)}) collective-permute-start(bf16[2,96,768]{2,1,0:T(8,128)(2,1)S(1)} %dynamic-slice_bitcast_fusion.8), channel_id=1, source_target_pairs={{0,8},{4,12},{8,0},{12,4},{16,24},{20,28},{24,16},{28,20},{1,9},{5... | collective-permute-start | bytes 884744 | tf_op jit(solution)/shard_map/ppermute | solution.py:19
  588.1 10.8 %collective-permute-start.26 = (bf16[2,24,1664]{2,1,0:T(8,128)(2,1)S(1)}, bf16[2,24,1664]{2,1,0:T(8,128)(2,1)S(1)}, u32[]{:S(2)}, u32[]{:S(2)}) collective-permute-start(bf16[2,24,1664]{2,1,0:T(8,128)(2,1)S(1)} %dynamic-slice_bitcast_fusion.11), channel_id=1, source_target_pairs={{0,8},{4,12},{8,0},{12,4},{16,24},{20,28},{24,16},{28,20},{1,9},{5... | collective-permute-start | bytes 479240 | tf_op jit(solution)/shard_map/ppermute | solution.py:19
  590.6 19.9 %collective-permute-start.31 = (bf16[2,24,3072]{2,1,0:T(8,128)(2,1)}, bf16[2,24,3072]{2,1,0:T(8,128)(2,1)}, u32[]{:S(2)}, u32[]{:S(2)}) collective-permute-start(bf16[2,24,3072]{2,1,0:T(8,128)(2,1)} %dynamic-slice_bitcast_fusion.9), channel_id=1, source_target_pairs={{0,8},{4,12},{8,0},{12,4},{16,24},{20,28},{24,16},{28,20},{1,9},{5... | collective-permute-start | bytes 884744 | tf_op jit(solution)/shard_map/ppermute | solution.py:19
  598.9 6.1 collective-permute-start.27
  600.5 11.3 %collective-permute-start.37 = (bf16[96,768]{1,0:T(8,128)(2,1)}, bf16[96,768]{1,0:T(8,128)(2,1)}, u32[]{:S(2)}, u32[]{:S(2)}) collective-permute-start(bf16[96,768]{1,0:T(8,128)(2,1)} %dynamic-slice_bitcast_fusion.12), channel_id=1, source_target_pairs={{0,16},{4,20},{8,24},{12,28},{16,0},{20,4},{24,8},{28,12},{1,17},{... | collective-permute-start | bytes 442376 | tf_op jit(solution)/shard_map/ppermute | solution.py:19
  611.6 6.9 %collective-permute-start.32 = (bf16[24,3072]{1,0:T(8,128)(2,1)S(1)}, bf16[24,3072]{1,0:T(8,128)(2,1)S(1)}, u32[]{:S(2)}, u32[]{:S(2)}) collective-permute-start(bf16[24,3072]{1,0:T(8,128)(2,1)S(1)} %dynamic-slice_bitcast_fusion.13), channel_id=1, source_target_pairs={{0,16},{4,20},{8,24},{12,28},{16,0},{20,4},{24,8},{28,12},{1,17},{... | collective-permute-start | bytes 442376 | tf_op jit(solution)/shard_map/ppermute | solution.py:19
  (101 other events, 605.8 us)
